TPU v7x, 32 devices: a whole 2x2x4 slice. The times are simulated.
32 devices in a mesh: frag: 8 (over z, y), blk: 4 (over x, core).
Axes of the slice: x: 2, y: 2, z: 4, core: 2. Of those that a mesh axis runs over, the one named last changes fastest.
Arguments:
- amps: float32 [8, 128, 8, 128], P('frag', 'blk'), may hold values from -1.5 to 1.5
- exch: float32 [8, 128, 8, 128], P('frag', 'blk'), may hold values from -4 to 4
- factors: bfloat16 [8, 384, 128, 128], P('frag', 'blk'), may hold values from -0.109375 to 0.109375
- occupied_pair_ladder: float32 [8, 8, 8], P('frag'), may hold values from -1 to 1
- virtual_fock_block: float32 [8, 128, 128], P('frag'), may hold values from -0.1875 to 0.1875
- virtual_orbital_energy: float32 [8, 128], P('frag'), may hold values from 1 to 3
- pair_energy: float32 [8, 8], P('frag'), may hold values from -1.5 to -0.5
- energy_weight: int32 [8, 8], P('frag'), may hold values from 0 to 2
- export_rows: int32 [8, 2, 2], P('frag'), may hold values from 2 to 5, as said below
Outputs:
- new_amps: float32 [8, 128, 8, 128], P('frag', 'blk')
- res_norms: float32 [8, 2], P('frag')
- energy: float32 [], replicated
Inputs may be any that keep to these rules, and one draw needn't show every extreme that they name: `export_rows`: for each fragment the 4 entries are distinct core rows.
All inputs are finite; a program needn't handle non-finite values.
Results may differ from a plain program's by a relative error of at most 0.0009.
Values may be sent and summed in bfloat16 or wider, within the bound.
No kernel may reach another device: no remote copies, remote signals or barrier semaphores. Data moves between devices by JAX's collectives and lax.ppermute only.
A program may use at most 128 MiB of HBM per device.

v0:
```python
import functools

import jax
import jax.numpy as jnp
from jax import lax
from jax.experimental import pallas as pl
from jax.experimental.pallas import tpu as pltpu
from jax.sharding import PartitionSpec as P

PASSES = 2
CROSS = 3
F32 = jnp.float32
BF16 = jnp.bfloat16

VMEM = pl.BlockSpec(memory_space=pltpu.VMEM)
SMEM = pl.BlockSpec(memory_space=pltpu.SMEM)
HBM = pl.BlockSpec(memory_space=pltpu.HBM)


def swap(value, step):
    count = lax.axis_size("blk")
    return lax.ppermute(value, "blk", [(at, at ^ step) for at in range(count)])


def even_swap(value):
    count = lax.axis_size("frag")
    return lax.ppermute(value, "frag", [(at, at ^ 1) for at in range(count)])


def odd_swap(value, closed):
    count = lax.axis_size("frag")
    links = []
    for at in range(count):
        to = at + (1 if at % 2 else -1)
        links.append((at, to % count if closed or 0 <= to < count else at))
    return lax.ppermute(value, "frag", links)


def wide_swap(value, frag_step):
    count = lax.axis_size("blk")
    links = [
        (f * count + b, (f ^ frag_step) * count + (b ^ 1))
        for f in range(lax.axis_size("frag"))
        for b in range(count)
    ]
    return lax.ppermute(value, ("frag", "blk"), links)


def call(body, out_shape, specs, *args, scratch=(), limit=6, flops=0):
    args = [
        pltpu.with_memory_space_constraint(arg, pltpu.HBM) if spec is HBM else arg
        for spec, arg in zip(specs, args, strict=True)
    ]
    return pl.pallas_call(
        body,
        out_shape=out_shape,
        in_specs=specs,
        out_specs=jax.tree.map(lambda _: VMEM, out_shape),
        scratch_shapes=scratch,
        cost_estimate=pl.CostEstimate(flops=flops, bytes_accessed=0, transcendentals=0),
        compiler_params=pltpu.CompilerParams(vmem_limit_bytes=limit * 2**20),
    )(*args)


def shaped(*dims, dtype=F32):
    return jax.ShapeDtypeStruct(dims, dtype)


def times_fock(amp, fock):
    return lax.dot_general(
        amp,
        fock,
        (((1,), (1,)), ((), ())),
        precision=lax.Precision.HIGHEST,
        preferred_element_type=F32,
    )


def join(keep_first, keep, came):
    return jnp.where(
        keep_first,
        jnp.concatenate([keep, came], axis=0),
        jnp.concatenate([came, keep], axis=0),
    )


def early_body(
    meta,
    amps_in,
    exch_in,
    fock_in,
    eps_in,
    occ_in,
    pair_in,
    weight_in,
    low_keep,
    low_send,
    amps,
    exch,
    fock,
    eps,
    occ,
    pair,
    weight,
    sems,
):
    moves = (
        (amps_in, amps),
        (exch_in, exch),
        (fock_in, fock),
        (eps_in, eps),
        (occ_in, occ),
        (pair_in, pair),
        (weight_in, weight),
    )
    copies = [pltpu.make_async_copy(*move, sems.at[at]) for at, move in enumerate(moves)]
    for copy in copies:
        copy.start()
    copies[0].wait()
    half_count = amps.shape[1] // 2
    half = meta[2]
    for p in range(half_count):
        first = amps[:, p, :].astype(BF16)
        second = amps[:, half_count + p, :].astype(BF16)
        low_keep[p] = jnp.where(half == 0, first, second)
        low_send[p] = jnp.where(half == 0, second, first)
    for copy in copies[1:]:
        copy.wait()


def open_body(
    meta,
    occ,
    pair,
    weight,
    amps,
    exch,
    fock,
    eps,
    keep,
    send,
    level,
    fock_low,
    own,
    even_weights,
    odd_weights,
):
    rows, pairs, _ = amps.shape
    half_count = pairs // 2
    border = even_weights.shape[0]
    half = meta[2]
    at_start, at_end = meta[3] == 0, meta[3] == meta[4]
    is_even = meta[3] % 2 == 0
    wide = jnp.broadcast_to(eps[...], level.shape)
    level[...] = wide + wide.T
    levels = level[pl.ds(pl.multiple_of(meta[5] * rows, rows), rows), :]
    amp = [amps[:, p, :] for p in range(pairs)]
    turned = times_fock(jnp.concatenate(amp, axis=0), fock[...])
    for p in range(pairs):
        integral = exch[:, p, :]
        partial = integral + turned[p * rows : (p + 1) * rows]
        for r in range(pairs):
            partial = partial + occ[p, r] * amp[r]
        base = partial - (levels - pair[0, p]) * amp[p]
        at = p % half_count

        @pl.when(half == p // half_count)
        def _():
            keep[0, at], keep[1, at], keep[2, at] = integral, base, partial

        @pl.when(half != p // half_count)
        def _():
            send[0, at], send[1, at], send[2, at] = integral, base, partial

        weighted = (weight[0, p].astype(F32) * 0.5) * integral
        if p < border:

            @pl.when(is_even)
            def _():
                odd_weights[p] = weighted

            @pl.when(jnp.logical_not(is_even))
            def _():
                even_weights[p] = weighted

            weighted = jnp.where(at_start, weighted, 0.0)
        if p >= pairs - border:

            @pl.when(is_even)
            def _():
                even_weights[p - (pairs - border)] = weighted

            @pl.when(jnp.logical_not(is_even))
            def _():
                odd_weights[p - (pairs - border)] = weighted

            weighted = jnp.where(at_end, weighted, 0.0)
        own[p] = weighted

    scaled = fock[...] * 0.5
    high = scaled.astype(BF16)
    fock_low[0] = high
    fock_low[1] = (scaled - high.astype(F32)).astype(BF16)


def hole_body(meta, occ, pair, amp, from_mate, keep, came, fock, level, base):
    half_count, rows, virt = amp.shape
    core, chip, half = meta[0], meta[1], meta[2]
    turned = times_fock(amp[...].reshape(half_count * rows, virt), fock[...])
    levels = level[pl.ds(pl.multiple_of(chip * rows, rows), rows), :]
    for p in range(half_count):
        at = half * half_count + p
        total = join(core == 0, keep[0, p], came[0, p])
        total = total + turned[p * rows : (p + 1) * rows] - (levels - pair[0, at]) * amp[p]
        for r in range(half_count):
            total = total + occ[at, half * half_count + r] * amp[r]
            total = total + occ[at, (1 - half) * half_count + r] * from_mate[r, :rows, :]
        base[p] = total


def ladder_body(meta, fock_low, *rest, group, count):
    lows, (source, far), rest = rest[:count], rest[count : count + 2], rest[count + 2 :]
    closing = count == 1
    if not closing:
        (keep, came), rest = rest[:2], rest[2:]
    outs, (near, gathered, turned, half_done, total, sem) = rest[:-6], rest[-6:]
    fetch = pltpu.make_async_copy(source, near, sem)
    fetch.start()
    half_count, rows, virt = lows[0].shape
    steps = far.shape[0] // group
    chip = meta[1]
    if count == 1:
        gathered = lows[0]
    else:
        for low, offset in zip(lows, (0, 1, CROSS, CROSS ^ 1), strict=True):
            at = jnp.bitwise_xor(meta[5], offset)
            gathered[:, pl.ds(pl.multiple_of(at * rows, rows), rows), :] = low[...]
    rows = virt // 2
    for p in range(half_count):
        turned[p * virt : (p + 1) * virt] = gathered[p].astype(F32).T.astype(BF16)

    contract_last = (((1,), (1,)), ((), ()))

    def first_half(slab, at, slot):
        for j in range(group // 2):
            two = slab[pl.ds(at * group + 2 * j, 2)].reshape(2 * virt, virt)
            part = lax.dot_general(
                turned[...], two, contract_last, preferred_element_type=F32
            ).astype(BF16)
            for p in range(half_count):
                for q in range(2):
                    half_done[
                        slot,
                        (2 * j + q) * virt : (2 * j + q + 1) * virt,
                        p * virt : (p + 1) * virt,
                    ] = part[p * virt : (p + 1) * virt, q * virt : (q + 1) * virt]

    def second_half(slab, at, slot):
        across = jnp.concatenate([slab[at * group + q] for q in range(group)], axis=1)
        total[...] += jnp.dot(across, half_done[slot], preferred_element_type=F32)

    fock_part = lax.dot_general(
        turned[...],
        fock_low[...].reshape(2 * virt, virt),
        contract_last,
        preferred_element_type=F32,
    )
    for p in range(half_count):
        block = fock_part[p * virt : (p + 1) * virt]
        total[:, p * virt : (p + 1) * virt] = block[:, :virt] + block[:, virt:]

    def sweep(slab, offset):
        def step(at, carry):
            second_half(slab, at - 1, (offset + at - 1) % 2)
            first_half(slab, at, (offset + at) % 2)
            return carry

        lax.fori_loop(1, steps, step, 0)

    first_half(far, 0, 0)
    sweep(far, 0)
    fetch.wait()
    second_half(far, steps - 1, (steps - 1) % 2)
    first_half(near, 0, steps % 2)
    sweep(near, steps)
    second_half(near, steps - 1, (2 * steps - 1) % 2)
    for p in range(half_count):
        block = total[:, p * virt : (p + 1) * virt].T
        top, bottom = block[:rows], block[rows:]
        if closing:
            send, kept = outs
            kept[p] = jnp.where(chip == 0, top, bottom)
            send[p] = jnp.where(chip == 0, bottom, top).astype(BF16)
        else:
            part, send = outs
            part[p] = block
            extra = join(meta[0] == 0, keep[2, p], came[2, p])
            send[p, :rows, :] = (top + jnp.where(chip == 0, extra, 0.0)).astype(BF16)
            send[p, rows:, :] = (bottom + jnp.where(chip == 0, 0.0, extra)).astype(BF16)


def ladder(meta, fock_low, lows, near, far, *own):
    half_count, _, virt = lows[0].shape
    rows = virt // 2
    aux = near.shape[0]
    group = max(g for g in range(2, 50, 2) if aux % g == 0)
    if own:
        out = (shaped(half_count, virt, virt), shaped(half_count, virt, virt, dtype=BF16))
    else:
        out = (shaped(half_count, rows, virt, dtype=BF16), shaped(half_count, rows, virt))
    return call(
        functools.partial(ladder_body, group=group, count=len(lows)),
        out,
        (SMEM,) + (VMEM,) * (1 + len(lows)) + (HBM, VMEM) + (VMEM,) * len(own),
        meta,
        fock_low,
        *lows,
        near,
        far,
        *own,
        scratch=(
            pltpu.VMEM((aux, virt, virt), BF16),
            pltpu.VMEM((half_count, virt, virt), BF16),
            pltpu.VMEM((half_count * virt, virt), BF16),
            pltpu.VMEM((2, group * virt, half_count * virt), BF16),
            pltpu.VMEM((virt, half_count * virt), F32),
            pltpu.SemaphoreType.DMA(()),
        ),
        limit=28,
        flops=8 * aux * half_count * virt**3,
    )


def fold_squares(residual):
    rows, virt = residual.shape
    return jnp.sum((residual * residual).reshape(rows // 8, 8, virt), axis=0)


def middle_body(
    meta,
    pair,
    picked,
    part,
    part_came,
    level,
    keep,
    came,
    own,
    even_came,
    odd_came,
    amp,
    low,
    squares,
    to_mate,
    keep_weights,
    weights,
):
    half_count, rows, _ = amp.shape
    core, chip, half = meta[0], meta[1], meta[2]
    mine = pl.ds(pl.multiple_of(chip * rows, rows), rows)
    other = pl.ds(pl.multiple_of((1 - chip) * rows, rows), rows)
    norm = jnp.zeros(squares.shape, F32)
    for p in range(half_count):
        shift_by = pair[0, half * half_count + p]
        lad = part[p, mine, :] + part_came[p, mine, :].astype(F32)
        fresh = (join(core == 0, keep[2, p], came[2, p]) + lad) / (level[mine, :] - shift_by)
        norm = norm + fold_squares(join(core == 0, keep[1, p], came[1, p]) + lad)
        amp[p] = fresh
        to_mate[p, :rows, :] = fresh
        low[p, mine, :] = fresh.astype(BF16)
        total = part[p, other, :] + part_came[p, other, :].astype(F32)
        low[p, other, :] = (total / (level[other, :] - shift_by)).astype(BF16)
    squares[...] = norm
    is_even, at_start, at_end = meta[3] % 2 == 0, meta[3] == 0, meta[3] == meta[4]
    weights[...] = own[...]
    for r in range(even_came.shape[0]):
        above = jnp.where(is_even, even_came[r], odd_came[r])
        below = jnp.where(is_even, odd_came[r], even_came[r])
        at = picked[0, r]
        weights[at] = weights[at] + jnp.where(at_end, 0.0, above)
        at = picked[1, r]
        weights[at] = weights[at] + jnp.where(at_start, 0.0, below)
    for p in range(half_count):
        keep_weights[p] = weights[half * half_count + p]
        to_mate[p, rows:, :] = weights[(1 - half) * half_count + p]


def last_body(
    meta, pair, part, came, level, base, amp, keep_weights, from_mate, first, keep, send, sums_out
):
    half_count, rows, virt = base.shape
    core, chip, half = meta[0], meta[1], meta[2]
    single = rows // 2
    levels = level[pl.ds(pl.multiple_of(chip * rows, rows), rows), :]
    norm = jnp.zeros(first.shape, F32)
    energy = jnp.zeros((single, virt), F32)
    for p in range(half_count):
        residual = base[p] + part[p] + came[p].astype(F32)
        norm = norm + fold_squares(residual)
        fresh = amp[p] + residual / (levels - pair[0, half * half_count + p])
        top, bottom = fresh[:single], fresh[single:]
        mine = jnp.where(core == 0, top, bottom)
        mate = jnp.where(core == 0, bottom, top)
        energy = energy + keep_weights[p] * mine + from_mate[p, rows:, :] * mate
        keep[p * single : (p + 1) * single, :] = mine
        send[p * single : (p + 1) * single, :] = mate
    tail = send.shape[0] - half_count * single
    slot = lax.broadcasted_iota(jnp.int32, (tail, virt), 0)
    sums = jnp.where(slot == 0, jnp.sum(energy), 0.0)
    sums = jnp.where(slot == 1, jnp.sum(first[...]), sums)
    sums = jnp.where(slot == 2, jnp.sum(norm), sums)
    keep[half_count * single :, :] = sums
    send[half_count * single :, :] = sums
    sums_out[...] = sums


def border_body(meta, picked, keep, came, whole, even_rows, odd_rows, sums):
    pairs, single, _ = whole.shape
    half_count = pairs // 2
    border = picked.shape[1]
    half = meta[2]
    for p in range(half_count):
        whole[half * half_count + p] = keep[p * single : (p + 1) * single, :]
        whole[(1 - half) * half_count + p] = came[p * single : (p + 1) * single, :]
    parity = meta[3] % 2
    for r in range(border):
        even_rows[r * single : (r + 1) * single, :] = whole[picked[parity, r]]
        odd_rows[r * single : (r + 1) * single, :] = whole[picked[1 - parity, r]]
    sums[...] = keep[half_count * single :, :] + came[half_count * single :, :]


def close_body(meta, whole, even_came, odd_came, squares, new, norms):
    norms[...] = jnp.sqrt(jnp.concatenate([squares[1:2, 0:1], squares[2:3, 0:1]], axis=1))
    pairs, single, _ = whole.shape
    border = (even_came.shape[0] - 8) // single
    is_even, at_start, at_end = meta[3] % 2 == 0, meta[3] == 0, meta[3] == meta[4]
    for p in range(pairs):
        row = whole[p]
        if p < border:
            block = slice(p * single, (p + 1) * single)
            left = jnp.where(is_even, odd_came[block, :], even_came[block, :])
            row = jnp.where(at_start, row, left)
        if p >= pairs - border:
            at = p - (pairs - border)
            block = slice(at * single, (at + 1) * single)
            right = jnp.where(is_even, even_came[block, :], odd_came[block, :])
            row = jnp.where(at_end, row, right)
        new[:, p, :] = row


def on_device(
    amps,
    exch,
    factors,
    occupied_pair_ladder,
    virtual_fock_block,
    virtual_orbital_energy,
    pair_energy,
    energy_weight,
    export_rows,
):
    _, row_count, pairs, virt = amps.shape
    half_count = pairs // 2
    both = 2 * row_count
    place = lax.axis_index("blk")
    core, chip = place % 2, place // 2
    half = core ^ chip if CROSS == 3 else core
    frag = lax.axis_index("frag")
    last = jnp.full_like(frag, lax.axis_size("frag") - 1)
    meta = jnp.stack([core, chip, half, frag, last, place]).astype(jnp.int32)
    occ, fock, pair = occupied_pair_ladder[0], virtual_fock_block[0], pair_energy[0]
    near = factors[0]

    border = export_rows.shape[2]
    edge = shaped(border, row_count, virt)
    single = shaped(half_count, row_count, virt)
    single_low = shaped(half_count, row_count, virt, dtype=BF16)
    triple = shaped(3, half_count, row_count, virt)
    low_keep, low_send, *near_inputs = call(
        early_body,
        (
            single_low,
            single_low,
            shaped(*amps.shape[1:]),
            shaped(*amps.shape[1:]),
            shaped(*fock.shape),
            shaped(*virtual_orbital_energy.shape),
            shaped(*occ.shape),
            shaped(*pair_energy.shape),
            shaped(*energy_weight.shape, dtype=jnp.int32),
        ),
        (SMEM,) + (HBM,) * 7,
        meta,
        amps[0],
        exch[0],
        fock,
        virtual_orbital_energy,
        occ,
        pair_energy,
        energy_weight,
        scratch=(pltpu.SemaphoreType.DMA((7,)),),
    )
    amps, exch, fock, eps, occ, pair, weight = near_inputs
    keep, send, level, fock_low, own_weights, even_weights, odd_weights = call(
        open_body,
        (
            triple,
            triple,
            shaped(virt, virt),
            shaped(2, virt, virt, dtype=BF16),
            shaped(pairs, row_count, virt),
            edge,
            edge,
        ),
        (SMEM,) * 4 + (VMEM,) * 4,
        meta,
        occ,
        pair,
        weight,
        amps,
        exch,
        fock,
        eps,
    )
    lows = [low_keep]
    for value, step in ((low_send, 1), (low_keep, CROSS), (low_send, CROSS ^ 1)):
        lows.append(swap(value, step))
    far = swap(near, 1)
    came = swap(send, 1)
    came = swap(send, 1)
    far_keep = swap(keep[2], CROSS)
    far_came = swap(send[2], CROSS ^ 1)
    odd_came = odd_swap(odd_weights, False)
    own = shaped(half_count, both, virt)
    part, send = ladder(meta, fock_low, lows, near, far, keep, came)
    send, even_weights, odd_weights = lax.optimization_barrier((send, even_weights, odd_weights))
    part_came = swap(send, CROSS)
    even_came = even_swap(even_weights)
    odd_came = odd_swap(odd_weights, False)
    small = shaped(8, virt)
    low = shaped(half_count, virt, virt, dtype=BF16)
    amp, low, first, to_mate, keep_weights = call(
        middle_body,
        (own, low, small, shaped(half_count, both + row_count, virt), single),
        (SMEM, SMEM, SMEM) + (VMEM,) * 8,
        meta,
        pair,
        export_rows[0],
        part,
        part_came,
        level,
        keep,
        came,
        own_weights,
        even_came,
        odd_came,
        scratch=(pltpu.VMEM((pairs, row_count, virt), F32),),
    )
    from_mate = swap(to_mate, 1)
    send, part = ladder(meta, fock_low, (low,), near, far)
    part_came = swap(send, CROSS)
    base = call(
        hole_body,
        own,
        (SMEM, SMEM, SMEM) + (VMEM,) * 6,
        meta,
        occ,
        pair,
        amp,
        from_mate,
        keep,
        came,
        fock,
        level,
    )
    packed = shaped(half_count * row_count + 8, virt)
    last_keep, send, sums = call(
        last_body,
        (packed, packed, small),
        (SMEM, SMEM) + (VMEM,) * 8,
        meta,
        pair,
        part,
        part_came,
        level,
        base,
        amp,
        keep_weights,
        from_mate,
        first,
    )
    last_came = swap(send, 1)
    sum_cross = swap(sums, CROSS)
    sum_diag = swap(sums, CROSS ^ 1)
    rows = shaped(border * row_count, virt)
    whole, even_rows, odd_rows, sums = call(
        border_body,
        (shaped(pairs, row_count, virt), rows, rows, small),
        (SMEM, SMEM, VMEM, VMEM),
        meta,
        export_rows[0],
        last_keep,
        last_came,
    )
    sums = sums + (sum_cross + sum_diag)
    norm_squares = sums
    even_came = even_swap(jnp.concatenate([even_rows, sums], axis=0))
    sums = sums + even_came[border * row_count :]
    odd_came = odd_swap(jnp.concatenate([odd_rows, sums], axis=0), True)
    sums = sums + odd_came[border * row_count :]
    step = 4
    while step < lax.axis_size("frag"):
        sums = sums + wide_swap(sums, step)
        step *= 2
    new, norms = call(
        close_body,
        (shaped(row_count, pairs, virt), shaped(1, PASSES)),
        (SMEM, VMEM, VMEM, VMEM, VMEM),
        meta,
        whole,
        even_came,
        odd_came,
        norm_squares,
    )
    energy = -sums[0, 0] / (virt * virt)
    return new[None], norms, energy


def solution(mesh):
    placed = (
        P("frag", "blk", None, None),
        P("frag", "blk", None, None),
        P("frag", "blk", None, None),
        P("frag", None, None),
        P("frag", None, None),
        P("frag", None),
        P("frag", None),
        P("frag", None),
        P("frag", None, None),
    )

    return jax.shard_map(
        on_device,
        mesh=mesh,
        in_specs=placed,
        out_specs=(P("frag", "blk", None, None), P("frag", None), P()),
        check_vma=False,
    )
```

profile of v0, /device:TPU:0, one launch (start us, length us, event | category | flops | bytes accessed | tf_op | source)
XLA Modules:
  0.0 67.7 jit_solution(2327473764138640278)
XLA Ops:
  0.6 0.6 collective-permute-start.3
  1.2 0.1 stack.23.meta
  1.3 1.7 %shard_map.112 = (bf16[4,32,128]{2,1,0:T(8,128)(2,1)S(1)}, bf16[4,32,128]{2,1,0:T(8,128)(2,1)S(1)}, f32[32,8,128]{2,1,0:T(8,128)S(1)}, f32[32,8,128]{2,1,0:T(8,1...) custom-call(s32[6]{0:T(128)S(1)} %stack.23.meta, ...), custom_call_target="tpu_custom_call" | custom-call | tf_op jit(solution)/shard_map/pallas_call | solution.py:54
  3.0 2.0 %shard_map.113 = (f32[3,4,32,128]{3,2,1,0:T(8,128)S(1)}, f32[3,4,32,128]{3,2,1,0:T(8,128)S(1)}, f32[128,128]{1,0:T(8,128)S(1)}, bf16[2,128,128]{2,1,0:T(8,128)(2...) custom-call(s32[6]{0:T(128)S(1)} %stack.23.meta, ...), custom_call_target="tpu_custom_call" | custom-call | tf_op jit(solution)/shard_map/pallas_call | solution.py:54
  5.0 0.1 collective-permute-start.4
  5.1 2.6 %collective-permute-start.1 = (bf16[4,32,128]{2,1,0:T(8,128)(2,1)S(1)}, bf16[4,32,128]{2,1,0:T(8,128)(2,1)S(1)}, u32[]{:S(2)}, u32[]{:S(2)}) collective-permute-start(bf16[4,32,128]{2,1,0:T(8,128)(2,1)S(1)} %get-tuple-element.48.rest_0_), channel_id=1, source_target_pairs={{0,3},{1,2},{2,1},{3,0},{4,7},{5,6},{6,5},{7,4},{8,11},{9,10},{10,... | collective-permute-start | bytes 98312 | tf_op jit(solution)/shard_map/ppermute | solution.py:22
  7.7 0.3 collective-permute-start.2
  8.0 0.1 collective-permute-start
  8.2 1.3 %collective-permute-done.1.rest_2_ = bf16[4,32,128]{2,1,0:T(8,128)(2,1)S(1)} collective-permute-done((bf16[4,32,128]{2,1,0:T(8,128)(2,1)S(1)}, bf16[4,32,128]{2,1,0:T(8,128)(2,1)S(1)}, u32[]{:S(2)}, u32[]{:S(2)}) %collective-permute-start.1) | collective-permute-done | bytes 32800 | tf_op jit(solution)/shard_map/ppermute | solution.py:22
  9.5 2.1 %collective-permute-done.2.rest_3_ = bf16[4,32,128]{2,1,0:T(8,128)(2,1)S(1)} collective-permute-done((bf16[4,32,128]{2,1,0:T(8,128)(2,1)S(1)}, bf16[4,32,128]{2,1,0:T(8,128)(2,1)S(1)}, u32[]{:S(2)}, u32[]{:S(2)}) %collective-permute-start.2) | collective-permute-done | bytes 32800 | tf_op jit(solution)/shard_map/ppermute | solution.py:22
  11.6 0.0 collective-permute-done.rest_1_
  11.6 0.0 collective-permute-done.4.rest_7_.came
  11.6 0.0 collective-permute-done.3.rest_5_.rest_2_
  11.6 0.0 copy-start
  11.7 11.0 %shard_map.114 = (f32[4,128,128]{2,1,0:T(8,128)S(1)}, bf16[4,128,128]{2,1,0:T(8,128)(2,1)S(1)}) custom-call(s32[6]{0:T(128)S(1)} %stack.23.meta, bf16[2,128,128]{2,1,0:T(8,128)(2,1)S(1)} %get-tuple-element.47.fock_low, bf16[4,32,128]{2,1,0:T(8,128)(2,1)S(1)} %get-tuple-element.48.rest_0_, bf16[4,32,128]{2,1,0:T(8,128)(2,1)S(1)} %collective-permute-done.rest_1_, ...), custom_call_target="tpu_custom_call" | custom-call | flops 6442450944 | tf_op jit(solution)/shard_map/pallas_call | solution.py:54
  22.7 0.3 collective-permute-start.5
  23.0 1.5 %collective-permute-start.6 = (f32[2,32,128]{2,1,0:T(8,128)S(1)}, f32[2,32,128]{2,1,0:T(8,128)S(1)}, u32[]{:S(2)}, u32[]{:S(2)}) collective-permute-start(f32[2,32,128]{2,1,0:T(8,128)S(1)} %get-tuple-element.59), channel_id=1, source_target_pairs={{0,4},{4,0},{8,12},{12,8},{16,20},{20,16},{24,28},{28,24},{1,5},{5... | collective-permute-start | bytes 98312 | tf_op jit(solution)/shard_map/ppermute | solution.py:27
  24.5 0.8 %collective-permute-start.7 = (f32[2,32,128]{2,1,0:T(8,128)S(1)}, f32[2,32,128]{2,1,0:T(8,128)S(1)}, u32[]{:S(2)}, u32[]{:S(2)}) collective-permute-start(f32[2,32,128]{2,1,0:T(8,128)S(1)} %get-tuple-element.60), channel_id=1, source_target_pairs={{0,0},{4,8},{8,4},{12,16},{16,12},{20,24},{24,20},{28,28},{1,1},{5... | collective-permute-start | bytes 98312 | tf_op jit(solution)/shard_map/ppermute | solution.py:36
  25.4 1.6 %collective-permute-done.6.even_came = f32[2,32,128]{2,1,0:T(8,128)S(1)} collective-permute-done((f32[2,32,128]{2,1,0:T(8,128)S(1)}, f32[2,32,128]{2,1,0:T(8,128)S(1)}, u32[]{:S(2)}, u32[]{:S(2)}) %collective-permute-start.6) | collective-permute-done | bytes 32800 | tf_op jit(solution)/shard_map/ppermute | solution.py:27
  27.0 0.0 collective-permute-done.7.odd_came
  27.0 1.0 %collective-permute-done.5.part_came = bf16[4,128,128]{2,1,0:T(8,128)(2,1)S(1)} collective-permute-done((bf16[4,128,128]{2,1,0:T(8,128)(2,1)S(1)}, bf16[4,128,128]{2,1,0:T(8,128)(2,1)S(1)}, u32[]{:S(2)}, u32[]{:S(2)}) %collective-permute-start.5) | collective-permute-done | bytes 131104 | tf_op jit(solution)/shard_map/ppermute | solution.py:22
  28.0 0.0 copy-done
  28.0 0.7 shard_map.115
  28.7 0.1 collective-permute-start.9
  28.8 11.0 %shard_map.116 = (bf16[4,64,128]{2,1,0:T(8,128)(2,1)S(1)}, f32[4,64,128]{2,1,0:T(8,128)S(1)}) custom-call(s32[6]{0:T(128)S(1)} %stack.23.meta, bf16[2,128,128]{2,1,0:T(8,128)(2,1)S(1)} %get-tuple-element.47.fock_low, bf16[4,128,128]{2,1,0:T(8,128)(2,1)S(1)} %get-tuple-element.61.rest_0_, bf16[96,128,128]{2,1,0:T(8,128)(2,1)} %bitcast.21, ...), custom_call_target="tpu_custom_call" | custom-call | flops 6442450944 | tf_op jit(solution)/shard_map/pallas_call | solution.py:54
  39.8 1.5 %collective-permute-start.8 = (bf16[4,64,128]{2,1,0:T(8,128)(2,1)S(1)}, bf16[4,64,128]{2,1,0:T(8,128)(2,1)S(1)}, u32[]{:S(2)}, u32[]{:S(2)}) collective-permute-start(bf16[4,64,128]{2,1,0:T(8,128)(2,1)S(1)} %get-tuple-element.63), channel_id=1, source_target_pairs={{0,3},{1,2},{2,1},{3,0},{4,7},{5,6},{6,5},{7,4},{8,11},{9,10},{10,... | collective-permute-start | bytes 196616 | tf_op jit(solution)/shard_map/ppermute | solution.py:22
  41.3 0.0 collective-permute-done.9.from_mate
  41.3 0.9 %shard_map.117.base = f32[4,64,128]{2,1,0:T(8,128)S(1)} custom-call(s32[6]{0:T(128)S(1)} %stack.23.meta, f32[8,8]{1,0:T(8,128)S(1)} %get-tuple-element.41.occ, f32[1,8]{1,0:T(1,128)S(1)} %get-tuple-element.40.pair, f32[4,64,128]{2,1,0:T(8,128)S(1)} %get-tuple-element.64.amp, f32[4,96,128]{2,1,0:T(8,128)S(1)} %collective-permute-done.9.from_mate, ...), custom_call_target="tpu_custom_call" | custom-call | tf_op jit(solution)/shard_map/pallas_call | solution.py:54
  42.2 1.4 %collective-permute-done.8.came = bf16[4,64,128]{2,1,0:T(8,128)(2,1)S(1)} collective-permute-done((bf16[4,64,128]{2,1,0:T(8,128)(2,1)S(1)}, bf16[4,64,128]{2,1,0:T(8,128)(2,1)S(1)}, u32[]{:S(2)}, u32[]{:S(2)}) %collective-permute-start.8) | collective-permute-done | bytes 65568 | tf_op jit(solution)/shard_map/ppermute | solution.py:22
  43.6 0.7 %shard_map.118 = (f32[136,128]{1,0:T(8,128)S(1)}, f32[136,128]{1,0:T(8,128)S(1)}, f32[8,128]{1,0:T(8,128)S(1)}) custom-call(s32[6]{0:T(128)S(1)} %stack.23.meta, f32[1,8]{1,0:T(1,128)S(1)} %get-tuple-element.40.pair, f32[4,64,128]{2,1,0:T(8,128)S(1)} %get-tuple-element.62.part, bf16[4,64,128]{2,1,0:T(8,128)(2,1)S(1)} %collective-permute-done.8.came, ...), custom_call_target="tpu_custom_call" | custom-call | tf_op jit(solution)/shard_map/pallas_call | solution.py:54
  44.3 0.6 collective-permute-start.10
  44.9 1.4 %collective-permute-start.12 = (f32[8,128]{1,0:T(8,128)S(1)}, f32[8,128]{1,0:T(8,128)S(1)}, u32[]{:S(2)}, u32[]{:S(2)}) collective-permute-start(f32[8,128]{1,0:T(8,128)S(1)} %get-tuple-element.73), channel_id=1, source_target_pairs={{0,2},{1,3},{2,0},{3,1},{4,6},{5,7},{6,4},{7,5},{8,10},{9,11},{10,... | collective-permute-start | bytes 12296 | tf_op jit(solution)/shard_map/ppermute | solution.py:22
  46.3 0.0 collective-permute-start.11
  46.3 0.0 collective-permute-done.10.came
  46.3 0.6 shard_map.119
  46.9 1.6 %collective-permute-done.12 = f32[8,128]{1,0:T(8,128)S(1)} collective-permute-done((f32[8,128]{1,0:T(8,128)S(1)}, f32[8,128]{1,0:T(8,128)S(1)}, u32[]{:S(2)}, u32[]{:S(2)}) %collective-permute-start.12) | collective-permute-done | bytes 4128 | tf_op jit(solution)/shard_map/ppermute | solution.py:22
  48.5 0.9 %collective-permute-done.11 = f32[8,128]{1,0:T(8,128)S(1)} collective-permute-done((f32[8,128]{1,0:T(8,128)S(1)}, f32[8,128]{1,0:T(8,128)S(1)}, u32[]{:S(2)}, u32[]{:S(2)}) %collective-permute-start.11) | collective-permute-done | bytes 4128 | tf_op jit(solution)/shard_map/ppermute | solution.py:22
  49.3 3.4 %collective-permute-start.13 = (f32[72,128]{1,0:T(8,128)S(1)}, f32[72,128]{1,0:T(8,128)S(1)}, u32[]{:S(2)}, u32[]{:S(2)}) collective-permute-start(f32[72,128]{1,0:T(8,128)S(1)} %pad_maximum_fusion), channel_id=1, source_target_pairs={{0,4},{4,0},{8,12},{12,8},{16,20},{20,16},{24,28},{28,24},{1,5},{5... | collective-permute-start | bytes 110600 | tf_op jit(solution)/shard_map/ppermute | solution.py:27
  52.8 1.9 %collective-permute-done.13.even_came = f32[72,128]{1,0:T(8,128)S(1)} collective-permute-done((f32[72,128]{1,0:T(8,128)S(1)}, f32[72,128]{1,0:T(8,128)S(1)}, u32[]{:S(2)}, u32[]{:S(2)}) %collective-permute-start.13) | collective-permute-done | bytes 36896 | tf_op jit(solution)/shard_map/ppermute | solution.py:27
  54.7 4.6 %collective-permute-start.14 = (f32[72,128]{1,0:T(8,128)S(1)}, f32[72,128]{1,0:T(8,128)S(1)}, u32[]{:S(2)}, u32[]{:S(2)}) collective-permute-start(f32[72,128]{1,0:T(8,128)S(1)} %pad_maximum_fusion.1), channel_id=1, source_target_pairs={{0,28},{4,8},{8,4},{12,16},{16,12},{20,24},{24,20},{28,0},{1,29},{... | collective-permute-start | bytes 110600 | tf_op jit(solution)/shard_map/ppermute | solution.py:36
  59.3 2.1 %collective-permute-done.14.odd_came = f32[72,128]{1,0:T(8,128)S(1)} collective-permute-done((f32[72,128]{1,0:T(8,128)S(1)}, f32[72,128]{1,0:T(8,128)S(1)}, u32[]{:S(2)}, u32[]{:S(2)}) %collective-permute-start.14) | collective-permute-done | bytes 36896 | tf_op jit(solution)/shard_map/ppermute | solution.py:36
  61.4 0.0 collective-permute-start.15
  61.4 1.3 %shard_map.120 = (f32[32,8,128]{2,1,0:T(8,128)}, f32[1,2]{1,0:T(1,128)}) custom-call(s32[6]{0:T(128)S(1)} %stack.23.meta, f32[8,32,128]{2,1,0:T(8,128)S(1)} %get-tuple-element.70.whole, f32[72,128]{1,0:T(8,128)S(1)} %collective-permute-done.13.even_came, f32[72,128]{1,0:T(8,128)S(1)} %collective-permute-done.14.odd_came, f32[8,128]{1,0:T(8,128)S(1)} %add_add_fusion.squares), custom_call_target="tpu_custom_call" | custom-call | tf_op jit(solution)/shard_map/pallas_call | solution.py:54
  62.7 2.6 %collective-permute-done.15 = f32[8,128]{1,0:T(8,128)S(1)} collective-permute-done((f32[8,128]{1,0:T(8,128)S(1)}, f32[8,128]{1,0:T(8,128)S(1)}, u32[]{:S(2)}, u32[]{:S(2)}) %collective-permute-start.15) | collective-permute-done | bytes 4128 | tf_op jit(solution)/shard_map/ppermute | solution.py:46
  65.4 0.5 slice.11
  (6 shorter events, 0.0 us)
Async XLA Ops:
  0.6 11.0 %collective-permute-start.3 = (bf16[96,128,128]{2,1,0:T(8,128)(2,1)}, bf16[96,128,128]{2,1,0:T(8,128)(2,1)S(1)}, u32[]{:S(2)}, u32[]{:S(2)}) collective-permute-start(bf16[96,128,128]{2,1,0:T(8,128)(2,1)} %bitcast.19), channel_id=1, source_target_pairs={{0,1},{1,0},{2,3},{3,2},{4,5},{5,4},{6,7},{7,6},{8,9},{9,8},{10,11... | collective-permute-start | bytes 9437192 | tf_op jit(solution)/shard_map/ppermute | solution.py:22
  5.0 6.7 %collective-permute-start.4 = (f32[3,4,32,128]{3,2,1,0:T(8,128)S(1)}, f32[3,4,32,128]{3,2,1,0:T(8,128)S(1)}, u32[]{:S(2)}, u32[]{:S(2)}) collective-permute-start(f32[3,4,32,128]{3,2,1,0:T(8,128)S(1)} %get-tuple-element.51), channel_id=1, source_target_pairs={{0,1},{1,0},{2,3},{3,2},{4,5},{5,4},{6,7},{7,6},{8,9},{9,8},{10,11... | collective-permute-start | bytes 589832 | tf_op jit(solution)/shard_map/ppermute | solution.py:22
  5.1 4.4 %collective-permute-start.1 = (bf16[4,32,128]{2,1,0:T(8,128)(2,1)S(1)}, bf16[4,32,128]{2,1,0:T(8,128)(2,1)S(1)}, u32[]{:S(2)}, u32[]{:S(2)}) collective-permute-start(bf16[4,32,128]{2,1,0:T(8,128)(2,1)S(1)} %get-tuple-element.48.rest_0_), channel_id=1, source_target_pairs={{0,3},{1,2},{2,1},{3,0},{4,7},{5,6},{6,5},{7,4},{8,11},{9,10},{10,... | collective-permute-start | bytes 98312 | tf_op jit(solution)/shard_map/ppermute | solution.py:22
  7.7 3.9 %collective-permute-start.2 = (bf16[4,32,128]{2,1,0:T(8,128)(2,1)S(1)}, bf16[4,32,128]{2,1,0:T(8,128)(2,1)S(1)}, u32[]{:S(2)}, u32[]{:S(2)}) collective-permute-start(bf16[4,32,128]{2,1,0:T(8,128)(2,1)S(1)} %get-tuple-element.49), channel_id=1, source_target_pairs={{0,2},{1,3},{2,0},{3,1},{4,6},{5,7},{6,4},{7,5},{8,10},{9,11},{10,... | collective-permute-start | bytes 98312 | tf_op jit(solution)/shard_map/ppermute | solution.py:22
  8.0 3.6 %collective-permute-start = (bf16[4,32,128]{2,1,0:T(8,128)(2,1)S(1)}, bf16[4,32,128]{2,1,0:T(8,128)(2,1)S(1)}, u32[]{:S(2)}, u32[]{:S(2)}) collective-permute-start(bf16[4,32,128]{2,1,0:T(8,128)(2,1)S(1)} %get-tuple-element.49), channel_id=1, source_target_pairs={{0,1},{1,0},{2,3},{3,2},{4,5},{5,4},{6,7},{7,6},{8,9},{9,8},{10,11... | collective-permute-start | bytes 98312 | tf_op jit(solution)/shard_map/ppermute | solution.py:22
  11.6 16.4 %copy-start = (s32[1,2,2]{2,1,0:T(2,128)S(1)}, s32[1,2,2]{2,1,0:T(2,128)}, u32[]{:S(2)}) copy-start(s32[1,2,2]{2,1,0:T(2,128)} %param.17) | copy-start | bytes 52
  22.7 5.3 %collective-permute-start.5 = (bf16[4,128,128]{2,1,0:T(8,128)(2,1)S(1)}, bf16[4,128,128]{2,1,0:T(8,128)(2,1)S(1)}, u32[]{:S(2)}, u32[]{:S(2)}) collective-permute-start(bf16[4,128,128]{2,1,0:T(8,128)(2,1)S(1)} %get-tuple-element.56), channel_id=1, source_target_pairs={{0,3},{1,2},{2,1},{3,0},{4,7},{5,6},{6,5},{7,4},{8,11},{9,10},{10,... | collective-permute-start | bytes 393224 | tf_op jit(solution)/shard_map/ppermute | solution.py:22
  23.0 4.0 %collective-permute-start.6 = (f32[2,32,128]{2,1,0:T(8,128)S(1)}, f32[2,32,128]{2,1,0:T(8,128)S(1)}, u32[]{:S(2)}, u32[]{:S(2)}) collective-permute-start(f32[2,32,128]{2,1,0:T(8,128)S(1)} %get-tuple-element.59), channel_id=1, source_target_pairs={{0,4},{4,0},{8,12},{12,8},{16,20},{20,16},{24,28},{28,24},{1,5},{5... | collective-permute-start | bytes 98312 | tf_op jit(solution)/shard_map/ppermute | solution.py:27
  24.5 2.5 %collective-permute-start.7 = (f32[2,32,128]{2,1,0:T(8,128)S(1)}, f32[2,32,128]{2,1,0:T(8,128)S(1)}, u32[]{:S(2)}, u32[]{:S(2)}) collective-permute-start(f32[2,32,128]{2,1,0:T(8,128)S(1)} %get-tuple-element.60), channel_id=1, source_target_pairs={{0,0},{4,8},{8,4},{12,16},{16,12},{20,24},{24,20},{28,28},{1,1},{5... | collective-permute-start | bytes 98312 | tf_op jit(solution)/shard_map/ppermute | solution.py:36
  28.7 12.6 %collective-permute-start.9 = (f32[4,96,128]{2,1,0:T(8,128)S(1)}, f32[4,96,128]{2,1,0:T(8,128)S(1)}, u32[]{:S(2)}, u32[]{:S(2)}) collective-permute-start(f32[4,96,128]{2,1,0:T(8,128)S(1)} %get-tuple-element.65), channel_id=1, source_target_pairs={{0,1},{1,0},{2,3},{3,2},{4,5},{5,4},{6,7},{7,6},{8,9},{9,8},{10,11... | collective-permute-start | bytes 589832 | tf_op jit(solution)/shard_map/ppermute | solution.py:22
  39.8 3.8 %collective-permute-start.8 = (bf16[4,64,128]{2,1,0:T(8,128)(2,1)S(1)}, bf16[4,64,128]{2,1,0:T(8,128)(2,1)S(1)}, u32[]{:S(2)}, u32[]{:S(2)}) collective-permute-start(bf16[4,64,128]{2,1,0:T(8,128)(2,1)S(1)} %get-tuple-element.63), channel_id=1, source_target_pairs={{0,3},{1,2},{2,1},{3,0},{4,7},{5,6},{6,5},{7,4},{8,11},{9,10},{10,... | collective-permute-start | bytes 196616 | tf_op jit(solution)/shard_map/ppermute | solution.py:22
  44.3 2.0 %collective-permute-start.10 = (f32[136,128]{1,0:T(8,128)S(1)}, f32[136,128]{1,0:T(8,128)S(1)}, u32[]{:S(2)}, u32[]{:S(2)}) collective-permute-start(f32[136,128]{1,0:T(8,128)S(1)} %get-tuple-element.69), channel_id=1, source_target_pairs={{0,1},{1,0},{2,3},{3,2},{4,5},{5,4},{6,7},{7,6},{8,9},{9,8},{10,11... | collective-permute-start | bytes 208904 | tf_op jit(solution)/shard_map/ppermute | solution.py:22
  44.9 3.6 %collective-permute-start.12 = (f32[8,128]{1,0:T(8,128)S(1)}, f32[8,128]{1,0:T(8,128)S(1)}, u32[]{:S(2)}, u32[]{:S(2)}) collective-permute-start(f32[8,128]{1,0:T(8,128)S(1)} %get-tuple-element.73), channel_id=1, source_target_pairs={{0,2},{1,3},{2,0},{3,1},{4,6},{5,7},{6,4},{7,5},{8,10},{9,11},{10,... | collective-permute-start | bytes 12296 | tf_op jit(solution)/shard_map/ppermute | solution.py:22
  46.3 3.1 %collective-permute-start.11 = (f32[8,128]{1,0:T(8,128)S(1)}, f32[8,128]{1,0:T(8,128)S(1)}, u32[]{:S(2)}, u32[]{:S(2)}) collective-permute-start(f32[8,128]{1,0:T(8,128)S(1)} %get-tuple-element.73), channel_id=1, source_target_pairs={{0,3},{1,2},{2,1},{3,0},{4,7},{5,6},{6,5},{7,4},{8,11},{9,10},{10,... | collective-permute-start | bytes 12296 | tf_op jit(solution)/shard_map/ppermute | solution.py:22
  49.3 5.4 %collective-permute-start.13 = (f32[72,128]{1,0:T(8,128)S(1)}, f32[72,128]{1,0:T(8,128)S(1)}, u32[]{:S(2)}, u32[]{:S(2)}) collective-permute-start(f32[72,128]{1,0:T(8,128)S(1)} %pad_maximum_fusion), channel_id=1, source_target_pairs={{0,4},{4,0},{8,12},{12,8},{16,20},{20,16},{24,28},{28,24},{1,5},{5... | collective-permute-start | bytes 110600 | tf_op jit(solution)/shard_map/ppermute | solution.py:27
  54.7 6.7 %collective-permute-start.14 = (f32[72,128]{1,0:T(8,128)S(1)}, f32[72,128]{1,0:T(8,128)S(1)}, u32[]{:S(2)}, u32[]{:S(2)}) collective-permute-start(f32[72,128]{1,0:T(8,128)S(1)} %pad_maximum_fusion.1), channel_id=1, source_target_pairs={{0,28},{4,8},{8,4},{12,16},{16,12},{20,24},{24,20},{28,0},{1,29},{... | collective-permute-start | bytes 110600 | tf_op jit(solution)/shard_map/ppermute | solution.py:36
  61.4 3.9 %collective-permute-start.15 = (f32[8,128]{1,0:T(8,128)S(1)}, f32[8,128]{1,0:T(8,128)S(1)}, u32[]{:S(2)}, u32[]{:S(2)}) collective-permute-start(f32[8,128]{1,0:T(8,128)S(1)} %slice_add_fusion), channel_id=1, source_target_pairs={{0,17},{1,16},{2,19},{3,18},{4,21},{5,20},{6,23},{7,22},{8,25},{9,... | collective-permute-start | bytes 12296 | tf_op jit(solution)/shard_map/ppermute | solution.py:46
where the time goes:
time: 67.8 us; the launch traced here: 67.7 us
  Pallas kernels  29.9 us (44%)
  starting transfers between devices  17.9 us (26%)
  waiting for transfers between devices  16.7 us (25%)
  between operations  2.51 us (4%)
    pallas_call x9, Pallas kernels, call(): pl.pallas_call(body, out_shape=out_shape, in_specs=specs, out_specs=jax.t...  29.9 us
    ppermute x11, waiting for transfers between devices, swap(): return lax.ppermute(value, 'blk', [(at, at ^ step) for at in range(count)])  8.38 us
    ppermute x11, starting transfers between devices, swap(): return lax.ppermute(value, 'blk', [(at, at ^ step) for at in range(count)])  7.58 us
    ppermute x2, starting transfers between devices, odd_swap(): return lax.ppermute(value, 'frag', links)  5.43 us
    ppermute x2, starting transfers between devices, even_swap(): return lax.ppermute(value, 'frag', [(at, at ^ 1) for at in range(count)])  4.94 us
    ppermute x2, waiting for transfers between devices, even_swap(): return lax.ppermute(value, 'frag', [(at, at ^ 1) for at in range(count)])  3.55 us
    ppermute x1, waiting for transfers between devices, wide_swap(): return lax.ppermute(value, ('frag', 'blk'), links)  2.64 us
    ppermute x2, waiting for transfers between devices, odd_swap(): return lax.ppermute(value, 'frag', links)  2.11 us
  transfers between devices with their start and end apart: 16, of which 10 were waited for; matrix products, arithmetic and copies ran while one was open for 0% of the time, Pallas kernels for 26%

commit v1 on v0

--- a/solution.py
+++ b/solution.py
@@ -23,17 +23,17 @@
 
 
 def even_swap(value):
-    count = lax.axis_size("frag")
-    return lax.ppermute(value, "frag", [(at, at ^ 1) for at in range(count)])
+    return wide_swap(value, 1)
 
 
 def odd_swap(value, closed):
-    count = lax.axis_size("frag")
+    count, width = lax.axis_size("frag"), lax.axis_size("blk")
     links = []
-    for at in range(count):
-        to = at + (1 if at % 2 else -1)
-        links.append((at, to % count if closed or 0 <= to < count else at))
-    return lax.ppermute(value, "frag", links)
+    for f in range(count):
+        to = f + (1 if f % 2 else -1)
+        to = to % count if closed or 0 <= to < count else f
+        links += [(f * width + b, to * width + (b ^ 1)) for b in range(width)]
+    return lax.ppermute(value, ("frag", "blk"), links)
 
 
 def wide_swap(value, frag_step):
@@ -142,12 +142,12 @@
     level,
     fock_low,
     own,
-    even_weights,
-    odd_weights,
 ):
     rows, pairs, _ = amps.shape
     half_count = pairs // 2
-    border = even_weights.shape[0]
+    border = (send.shape[0] - 3 * half_count) // 2
+    even_at = 3 * half_count
+    odd_at = even_at + border
     half = meta[2]
     at_start, at_end = meta[3] == 0, meta[3] == meta[4]
     is_even = meta[3] % 2 == 0
@@ -166,34 +166,18 @@
 
         @pl.when(half == p // half_count)
         def _():
-            keep[0, at], keep[1, at], keep[2, at] = integral, base, partial
+            keep[at], keep[half_count + at], keep[2 * half_count + at] = integral, base, partial
 
         @pl.when(half != p // half_count)
         def _():
-            send[0, at], send[1, at], send[2, at] = integral, base, partial
+            send[at], send[half_count + at], send[2 * half_count + at] = integral, base, partial
 
         weighted = (weight[0, p].astype(F32) * 0.5) * integral
         if p < border:
-
-            @pl.when(is_even)
-            def _():
-                odd_weights[p] = weighted
-
-            @pl.when(jnp.logical_not(is_even))
-            def _():
-                even_weights[p] = weighted
-
+            send[jnp.where(is_even, odd_at, even_at) + p] = weighted
             weighted = jnp.where(at_start, weighted, 0.0)
         if p >= pairs - border:
-
-            @pl.when(is_even)
-            def _():
-                even_weights[p - (pairs - border)] = weighted
-
-            @pl.when(jnp.logical_not(is_even))
-            def _():
-                odd_weights[p - (pairs - border)] = weighted
-
+            send[jnp.where(is_even, even_at, odd_at) + (p - (pairs - border))] = weighted
             weighted = jnp.where(at_end, weighted, 0.0)
         own[p] = weighted
 
@@ -210,7 +194,7 @@
     levels = level[pl.ds(pl.multiple_of(chip * rows, rows), rows), :]
     for p in range(half_count):
         at = half * half_count + p
-        total = join(core == 0, keep[0, p], came[0, p])
+        total = join(core == 0, keep[p], came[p])
         total = total + turned[p * rows : (p + 1) * rows] - (levels - pair[0, at]) * amp[p]
         for r in range(half_count):
             total = total + occ[at, half * half_count + r] * amp[r]
@@ -294,7 +278,7 @@
         else:
             part, send = outs
             part[p] = block
-            extra = join(meta[0] == 0, keep[2, p], came[2, p])
+            extra = join(meta[0] == 0, keep[2 * half_count + p], came[2 * half_count + p])
             send[p, :rows, :] = (top + jnp.where(chip == 0, extra, 0.0)).astype(BF16)
             send[p, rows:, :] = (bottom + jnp.where(chip == 0, 0.0, extra)).astype(BF16)
 
@@ -363,8 +347,8 @@
     for p in range(half_count):
         shift_by = pair[0, half * half_count + p]
         lad = part[p, mine, :] + part_came[p, mine, :].astype(F32)
-        fresh = (join(core == 0, keep[2, p], came[2, p]) + lad) / (level[mine, :] - shift_by)
-        norm = norm + fold_squares(join(core == 0, keep[1, p], came[1, p]) + lad)
+        fresh = (join(core == 0, keep[2 * half_count + p], came[2 * half_count + p]) + lad) / (level[mine, :] - shift_by)
+        norm = norm + fold_squares(join(core == 0, keep[half_count + p], came[half_count + p]) + lad)
         amp[p] = fresh
         to_mate[p, :rows, :] = fresh
         low[p, mine, :] = fresh.astype(BF16)
@@ -386,7 +370,7 @@
 
 
 def last_body(
-    meta, pair, part, came, level, base, amp, keep_weights, from_mate, first, keep, send, sums_out
+    meta, pair, part, came, level, base, amp, keep_weights, from_mate, first, packed, sums_out
 ):
     half_count, rows, virt = base.shape
     core, chip, half = meta[0], meta[1], meta[2]
@@ -402,31 +386,34 @@
         mine = jnp.where(core == 0, top, bottom)
         mate = jnp.where(core == 0, bottom, top)
         energy = energy + keep_weights[p] * mine + from_mate[p, rows:, :] * mate
-        keep[p * single : (p + 1) * single, :] = mine
-        send[p * single : (p + 1) * single, :] = mate
-    tail = send.shape[0] - half_count * single
-    slot = lax.broadcasted_iota(jnp.int32, (tail, virt), 0)
+        packed[p * single : (p + 1) * single, :] = mine
+        packed[(half_count + p) * single : (half_count + p + 1) * single, :] = mate
+    slot = lax.broadcasted_iota(jnp.int32, sums_out.shape, 0)
     sums = jnp.where(slot == 0, jnp.sum(energy), 0.0)
     sums = jnp.where(slot == 1, jnp.sum(first[...]), sums)
     sums = jnp.where(slot == 2, jnp.sum(norm), sums)
-    keep[half_count * single :, :] = sums
-    send[half_count * single :, :] = sums
+    packed[2 * half_count * single :, :] = sums
     sums_out[...] = sums
 
 
-def border_body(meta, picked, keep, came, whole, even_rows, odd_rows, sums):
+def border_body(meta, picked, packed, came, whole, even_rows, odd_rows, sums, mate):
     pairs, single, _ = whole.shape
     half_count = pairs // 2
-    border = picked.shape[1]
     half = meta[2]
-    for p in range(half_count):
-        whole[half * half_count + p] = keep[p * single : (p + 1) * single, :]
-        whole[(1 - half) * half_count + p] = came[p * single : (p + 1) * single, :]
+    mine_at = half * half_count
+    mate_at = (1 - half) * half_count
+    for p in range(half_count):
+        first = slice(p * single, (p + 1) * single)
+        second = slice((half_count + p) * single, (half_count + p + 1) * single)
+        whole[mine_at + p] = packed[first, :]
+        whole[mate_at + p] = came[second, :]
+        mate[mine_at + p] = packed[second, :]
+        mate[mate_at + p] = came[first, :]
     parity = meta[3] % 2
-    for r in range(border):
-        even_rows[r * single : (r + 1) * single, :] = whole[picked[parity, r]]
-        odd_rows[r * single : (r + 1) * single, :] = whole[picked[1 - parity, r]]
-    sums[...] = keep[half_count * single :, :] + came[half_count * single :, :]
+    for r in range(picked.shape[1]):
+        even_rows[r * single : (r + 1) * single, :] = mate[picked[parity, r]]
+        odd_rows[r * single : (r + 1) * single, :] = mate[picked[1 - parity, r]]
+    sums[...] = packed[2 * half_count * single :, :] + came[2 * half_count * single :, :]
 
 
 def close_body(meta, whole, even_came, odd_came, squares, new, norms):
@@ -472,10 +459,8 @@
     near = factors[0]
 
     border = export_rows.shape[2]
-    edge = shaped(border, row_count, virt)
     single = shaped(half_count, row_count, virt)
     single_low = shaped(half_count, row_count, virt, dtype=BF16)
-    triple = shaped(3, half_count, row_count, virt)
     low_keep, low_send, *near_inputs = call(
         early_body,
         (
@@ -501,16 +486,14 @@
         scratch=(pltpu.SemaphoreType.DMA((7,)),),
     )
     amps, exch, fock, eps, occ, pair, weight = near_inputs
-    keep, send, level, fock_low, own_weights, even_weights, odd_weights = call(
+    keep, send, level, fock_low, own_weights = call(
         open_body,
         (
-            triple,
-            triple,
+            shaped(3 * half_count, row_count, virt),
+            shaped(3 * half_count + 2 * border, row_count, virt),
             shaped(virt, virt),
             shaped(2, virt, virt, dtype=BF16),
             shaped(pairs, row_count, virt),
-            edge,
-            edge,
         ),
         (SMEM,) * 4 + (VMEM,) * 4,
         meta,
@@ -527,13 +510,12 @@
         lows.append(swap(value, step))
     far = swap(near, 1)
     came = swap(send, 1)
-    came = swap(send, 1)
-    far_keep = swap(keep[2], CROSS)
-    far_came = swap(send[2], CROSS ^ 1)
-    odd_came = odd_swap(odd_weights, False)
     own = shaped(half_count, both, virt)
     part, send = ladder(meta, fock_low, lows, near, far, keep, came)
-    send, even_weights, odd_weights = lax.optimization_barrier((send, even_weights, odd_weights))
+    even_at = 3 * half_count
+    send, even_weights, odd_weights = lax.optimization_barrier(
+        (send, came[even_at : even_at + border], came[even_at + border :])
+    )
     part_came = swap(send, CROSS)
     even_came = even_swap(even_weights)
     odd_came = odd_swap(odd_weights, False)
@@ -573,10 +555,9 @@
         fock,
         level,
     )
-    packed = shaped(half_count * row_count + 8, virt)
-    last_keep, send, sums = call(
+    packed, sums = call(
         last_body,
-        (packed, packed, small),
+        (shaped(pairs * row_count + 8, virt), small),
         (SMEM, SMEM) + (VMEM,) * 8,
         meta,
         pair,
@@ -589,7 +570,7 @@
         from_mate,
         first,
     )
-    last_came = swap(send, 1)
+    last_came = swap(packed, 1)
     sum_cross = swap(sums, CROSS)
     sum_diag = swap(sums, CROSS ^ 1)
     rows = shaped(border * row_count, virt)
@@ -599,8 +580,9 @@
         (SMEM, SMEM, VMEM, VMEM),
         meta,
         export_rows[0],
-        last_keep,
+        packed,
         last_came,
+        scratch=(pltpu.VMEM((pairs, row_count, virt), F32),),
     )
     sums = sums + (sum_cross + sum_diag)
     norm_squares = sums

time: 67.8 us -> 65.3 us (0.963)
  waiting for transfers between devices: 16.7 us -> 13.8 us
    ppermute x1 -> x3, starting transfers between devices: 0.01 us -> 5.75 us  [wide_swap(): return lax.ppermute(value, ('frag', 'blk'), links)]
    ppermute x4 -> x2, starting transfers between devices: 10.4 us -> 4.8 us  [odd_swap(): return lax.ppermute(value, ('frag', 'blk'), links)]
    ppermute x4 -> x2, waiting for transfers between devices: 5.67 us -> 1.65 us  [odd_swap(): return lax.ppermute(value, ('frag', 'blk'), links)]
    ppermute x1 -> x3, waiting for transfers between devices: 2.64 us -> 3.75 us  [wide_swap(): return lax.ppermute(value, ('frag', 'blk'), links)]
  transfers between devices with their start and end apart: 16 -> 16, of which waited for: 10 -> 9; matrix products, arithmetic and copies ran while one was open for 0% -> 0% of each run, Pallas kernels for 26% -> 27%
where the time goes in v1:
time: 65.3 us; the launch traced here: 65.1 us
  Pallas kernels  30.1 us (46%)
  starting transfers between devices  18.1 us (28%)
  waiting for transfers between devices  13.8 us (21%)
  between operations  2.5 us (4%)
    pallas_call x9, Pallas kernels, call(): pl.pallas_call(body, out_shape=out_shape, in_specs=specs, out_specs=jax.t...  30.1 us
    ppermute x11, waiting for transfers between devices, swap(): return lax.ppermute(value, 'blk', [(at, at ^ step) for at in range(count)])  8.42 us
    ppermute x11, starting transfers between devices, swap(): return lax.ppermute(value, 'blk', [(at, at ^ step) for at in range(count)])  7.54 us
    ppermute x3, starting transfers between devices, wide_swap(): return lax.ppermute(value, ('frag', 'blk'), links)  5.75 us
    ppermute x2, starting transfers between devices, odd_swap(): return lax.ppermute(value, ('frag', 'blk'), links)  4.8 us
    ppermute x3, waiting for transfers between devices, wide_swap(): return lax.ppermute(value, ('frag', 'blk'), links)  3.75 us
    ppermute x2, waiting for transfers between devices, odd_swap(): return lax.ppermute(value, ('frag', 'blk'), links)  1.65 us
  transfers between devices with their start and end apart: 16, of which 9 were waited for; matrix products, arithmetic and copies ran while one was open for 0% of the time, Pallas kernels for 27%

profile of v1, /device:TPU:0, one launch (start us, length us, event | category | flops | bytes accessed | tf_op | source)
XLA Modules:
  0.0 65.1 jit_solution(15655390073756122522)
XLA Ops:
  0.6 0.6 collective-permute-start.3
  1.2 0.1 stack.23.meta
  1.3 1.7 %shard_map.112 = (bf16[4,32,128]{2,1,0:T(8,128)(2,1)S(1)}, bf16[4,32,128]{2,1,0:T(8,128)(2,1)S(1)}, f32[32,8,128]{2,1,0:T(8,128)S(1)}, f32[32,8,128]{2,1,0:T(8,1...) custom-call(s32[6]{0:T(128)S(1)} %stack.23.meta, ...), custom_call_target="tpu_custom_call" | custom-call | tf_op jit(solution)/shard_map/pallas_call | solution.py:54
  3.0 2.0 %shard_map.113 = (f32[12,32,128]{2,1,0:T(8,128)S(1)}, f32[16,32,128]{2,1,0:T(8,128)S(1)}, f32[128,128]{1,0:T(8,128)S(1)}, bf16[2,128,128]{2,1,0:T(8,128)(2,1)S(1)}, f32[8,32,128]{2,1,0:T(8,128)S(1)}) custom-call(s32[6]{0:T(128)S(1)} %stack.23.meta, f32[8,8]{1,0:T(8,128)S(1)} %get-tuple-element.38.occ, f32[1,8]{1,0:T(1,128)S(1)} %get-tuple-element.37.pair, ...), custom_call_target="tpu_custom_call" | custom-call | tf_op jit(solution)/shard_map/pallas_call | solution.py:54
  5.0 0.1 collective-permute-start.4
  5.1 2.9 %collective-permute-start.2 = (bf16[4,32,128]{2,1,0:T(8,128)(2,1)S(1)}, bf16[4,32,128]{2,1,0:T(8,128)(2,1)S(1)}, u32[]{:S(2)}, u32[]{:S(2)}) collective-permute-start(bf16[4,32,128]{2,1,0:T(8,128)(2,1)S(1)} %get-tuple-element.46), channel_id=1, source_target_pairs={{0,2},{1,3},{2,0},{3,1},{4,6},{5,7},{6,4},{7,5},{8,10},{9,11},{10,... | collective-permute-start | bytes 98312 | tf_op jit(solution)/shard_map/ppermute | solution.py:22
  8.0 0.0 collective-permute-start
  8.0 0.1 collective-permute-start.1
  8.1 0.0 collective-permute-done.4.rest_7_.came
  8.1 3.2 %collective-permute-done.1.rest_2_ = bf16[4,32,128]{2,1,0:T(8,128)(2,1)S(1)} collective-permute-done((bf16[4,32,128]{2,1,0:T(8,128)(2,1)S(1)}, bf16[4,32,128]{2,1,0:T(8,128)(2,1)S(1)}, u32[]{:S(2)}, u32[]{:S(2)}) %collective-permute-start.1) | collective-permute-done | bytes 32800 | tf_op jit(solution)/shard_map/ppermute | solution.py:22
  11.3 0.0 collective-permute-done.2.rest_3_
  11.3 0.0 collective-permute-done.rest_1_
  11.4 0.0 collective-permute-done.3.rest_5_.rest_2_
  11.4 0.0 copy-start
  11.4 11.0 %shard_map.114 = (f32[4,128,128]{2,1,0:T(8,128)S(1)}, bf16[4,128,128]{2,1,0:T(8,128)(2,1)S(1)}) custom-call(s32[6]{0:T(128)S(1)} %stack.23.meta, bf16[2,128,128]{2,1,0:T(8,128)(2,1)S(1)} %get-tuple-element.44.fock_low, bf16[4,32,128]{2,1,0:T(8,128)(2,1)S(1)} %get-tuple-element.45.rest_0_, bf16[4,32,128]{2,1,0:T(8,128)(2,1)S(1)} %collective-permute-done.rest_1_, ...), custom_call_target="tpu_custom_call" | custom-call | flops 6442450944 | tf_op jit(solution)/shard_map/pallas_call | solution.py:54
  22.4 0.6 collective-permute-start.5
  23.0 1.6 %collective-permute-start.6 = (f32[2,32,128]{2,1,0:T(8,128)S(1)}, f32[2,32,128]{2,1,0:T(8,128)S(1)}, u32[]{:S(2)}, u32[]{:S(2)}) collective-permute-start(f32[2,32,128]{2,1,0:T(8,128)S(1)} %get-tuple-element.54), channel_id=1, source_target_pairs={{0,5},{1,4},{2,7},{3,6},{4,1},{5,0},{6,3},{7,2},{8,13},{9,12},{10,... | collective-permute-start | bytes 98312 | tf_op jit(solution)/shard_map/ppermute | solution.py:46
  24.6 0.2 collective-permute-start.7
  24.8 1.6 %collective-permute-done.6.even_came = f32[2,32,128]{2,1,0:T(8,128)S(1)} collective-permute-done((f32[2,32,128]{2,1,0:T(8,128)S(1)}, f32[2,32,128]{2,1,0:T(8,128)S(1)}, u32[]{:S(2)}, u32[]{:S(2)}) %collective-permute-start.6) | collective-permute-done | bytes 32800 | tf_op jit(solution)/shard_map/ppermute | solution.py:46
  26.3 0.0 collective-permute-done.7.odd_came
  26.3 1.2 %collective-permute-done.5.part_came = bf16[4,128,128]{2,1,0:T(8,128)(2,1)S(1)} collective-permute-done((bf16[4,128,128]{2,1,0:T(8,128)(2,1)S(1)}, bf16[4,128,128]{2,1,0:T(8,128)(2,1)S(1)}, u32[]{:S(2)}, u32[]{:S(2)}) %collective-permute-start.5) | collective-permute-done | bytes 131104 | tf_op jit(solution)/shard_map/ppermute | solution.py:22
  27.6 0.0 copy-done
  27.6 0.7 %shard_map.115 = (f32[4,64,128]{2,1,0:T(8,128)S(1)}, bf16[4,128,128]{2,1,0:T(8,128)(2,1)S(1)}, f32[8,128]{1,0:T(8,128)S(1)}, f32[4,96,128]{2,1,0:T(8,128)S(1)}, f32[4,32,128]{2,1,0:T(8,128)S(1)}) custom-call(s32[6]{0:T(128)S(1)} %stack.23.meta, f32[1,8]{1,0:T(1,128)S(1)} %get-tuple-element.37.pair, s32[2,2]{1,0:T(2,128)S(1)} %bitcast.13, ...), custom_call_target="tpu_custom_call" | custom-call | tf_op jit(solution)/shard_map/pallas_call | solution.py:54
  28.3 0.6 collective-permute-start.9
  28.8 11.2 %shard_map.116 = (bf16[4,64,128]{2,1,0:T(8,128)(2,1)S(1)}, f32[4,64,128]{2,1,0:T(8,128)S(1)}) custom-call(s32[6]{0:T(128)S(1)} %stack.23.meta, bf16[2,128,128]{2,1,0:T(8,128)(2,1)S(1)} %get-tuple-element.44.fock_low, bf16[4,128,128]{2,1,0:T(8,128)(2,1)S(1)} %get-tuple-element.56.rest_0_, bf16[96,128,128]{2,1,0:T(8,128)(2,1)} %bitcast.21, ...), custom_call_target="tpu_custom_call" | custom-call | flops 6442450944 | tf_op jit(solution)/shard_map/pallas_call | solution.py:54
  40.0 0.7 %collective-permute-start.8 = (bf16[4,64,128]{2,1,0:T(8,128)(2,1)S(1)}, bf16[4,64,128]{2,1,0:T(8,128)(2,1)S(1)}, u32[]{:S(2)}, u32[]{:S(2)}) collective-permute-start(bf16[4,64,128]{2,1,0:T(8,128)(2,1)S(1)} %get-tuple-element.58), channel_id=1, source_target_pairs={{0,3},{1,2},{2,1},{3,0},{4,7},{5,6},{6,5},{7,4},{8,11},{9,10},{10,... | collective-permute-start | bytes 196616 | tf_op jit(solution)/shard_map/ppermute | solution.py:22
  40.8 0.0 collective-permute-done.9.from_mate
  40.8 0.9 %shard_map.117.base = f32[4,64,128]{2,1,0:T(8,128)S(1)} custom-call(s32[6]{0:T(128)S(1)} %stack.23.meta, f32[8,8]{1,0:T(8,128)S(1)} %get-tuple-element.38.occ, f32[1,8]{1,0:T(1,128)S(1)} %get-tuple-element.37.pair, f32[4,64,128]{2,1,0:T(8,128)S(1)} %get-tuple-element.59.amp, f32[4,96,128]{2,1,0:T(8,128)S(1)} %collective-permute-done.9.from_mate, ...), custom_call_target="tpu_custom_call" | custom-call | tf_op jit(solution)/shard_map/pallas_call | solution.py:54
  41.7 2.6 %collective-permute-done.8.came = bf16[4,64,128]{2,1,0:T(8,128)(2,1)S(1)} collective-permute-done((bf16[4,64,128]{2,1,0:T(8,128)(2,1)S(1)}, bf16[4,64,128]{2,1,0:T(8,128)(2,1)S(1)}, u32[]{:S(2)}, u32[]{:S(2)}) %collective-permute-start.8) | collective-permute-done | bytes 65568 | tf_op jit(solution)/shard_map/ppermute | solution.py:22
  44.3 0.7 %shard_map.118 = (f32[264,128]{1,0:T(8,128)S(1)}, f32[8,128]{1,0:T(8,128)S(1)}) custom-call(s32[6]{0:T(128)S(1)} %stack.23.meta, f32[1,8]{1,0:T(1,128)S(1)} %get-tuple-element.37.pair, f32[4,64,128]{2,1,0:T(8,128)S(1)} %get-tuple-element.57.part, bf16[4,64,128]{2,1,0:T(8,128)(2,1)S(1)} %collective-permute-done.8.came, ...), custom_call_target="tpu_custom_call" | custom-call | tf_op jit(solution)/shard_map/pallas_call | solution.py:54
  45.0 0.2 collective-permute-start.10
  45.2 0.6 collective-permute-start.12
  45.8 1.1 %collective-permute-start.11 = (f32[8,128]{1,0:T(8,128)S(1)}, f32[8,128]{1,0:T(8,128)S(1)}, u32[]{:S(2)}, u32[]{:S(2)}) collective-permute-start(f32[8,128]{1,0:T(8,128)S(1)} %get-tuple-element.67), channel_id=1, source_target_pairs={{0,3},{1,2},{2,1},{3,0},{4,7},{5,6},{6,5},{7,4},{8,11},{9,10},{10,... | collective-permute-start | bytes 12296 | tf_op jit(solution)/shard_map/ppermute | solution.py:22
  47.0 0.0 collective-permute-done.10.came
  47.0 0.6 shard_map.119
  47.5 1.3 %collective-permute-done.12 = f32[8,128]{1,0:T(8,128)S(1)} collective-permute-done((f32[8,128]{1,0:T(8,128)S(1)}, f32[8,128]{1,0:T(8,128)S(1)}, u32[]{:S(2)}, u32[]{:S(2)}) %collective-permute-start.12) | collective-permute-done | bytes 4128 | tf_op jit(solution)/shard_map/ppermute | solution.py:22
  48.8 0.1 collective-permute-done.11
  48.9 2.1 %collective-permute-start.13 = (f32[72,128]{1,0:T(8,128)S(1)}, f32[72,128]{1,0:T(8,128)S(1)}, u32[]{:S(2)}, u32[]{:S(2)}) collective-permute-start(f32[72,128]{1,0:T(8,128)S(1)} %pad_maximum_fusion), channel_id=1, source_target_pairs={{0,5},{1,4},{2,7},{3,6},{4,1},{5,0},{6,3},{7,2},{8,13},{9,12},{10,... | collective-permute-start | bytes 110600 | tf_op jit(solution)/shard_map/ppermute | solution.py:46
  50.9 1.6 %collective-permute-done.13.even_came = f32[72,128]{1,0:T(8,128)S(1)} collective-permute-done((f32[72,128]{1,0:T(8,128)S(1)}, f32[72,128]{1,0:T(8,128)S(1)}, u32[]{:S(2)}, u32[]{:S(2)}) %collective-permute-start.13) | collective-permute-done | bytes 36896 | tf_op jit(solution)/shard_map/ppermute | solution.py:46
  52.6 4.6 %collective-permute-start.14 = (f32[72,128]{1,0:T(8,128)S(1)}, f32[72,128]{1,0:T(8,128)S(1)}, u32[]{:S(2)}, u32[]{:S(2)}) collective-permute-start(f32[72,128]{1,0:T(8,128)S(1)} %pad_maximum_fusion.1), channel_id=1, source_target_pairs={{0,29},{1,28},{2,31},{3,30},{4,9},{5,8},{6,11},{7,10},{8,5},{9,4},... | collective-permute-start | bytes 110600 | tf_op jit(solution)/shard_map/ppermute | solution.py:36
  57.2 1.6 %collective-permute-done.14.odd_came = f32[72,128]{1,0:T(8,128)S(1)} collective-permute-done((f32[72,128]{1,0:T(8,128)S(1)}, f32[72,128]{1,0:T(8,128)S(1)}, u32[]{:S(2)}, u32[]{:S(2)}) %collective-permute-start.14) | collective-permute-done | bytes 36896 | tf_op jit(solution)/shard_map/ppermute | solution.py:36
  58.9 2.1 %collective-permute-start.15 = (f32[8,128]{1,0:T(8,128)S(1)}, f32[8,128]{1,0:T(8,128)S(1)}, u32[]{:S(2)}, u32[]{:S(2)}) collective-permute-start(f32[8,128]{1,0:T(8,128)S(1)} %slice_add_fusion), channel_id=1, source_target_pairs={{0,17},{1,16},{2,19},{3,18},{4,21},{5,20},{6,23},{7,22},{8,25},{9,... | collective-permute-start | bytes 12296 | tf_op jit(solution)/shard_map/ppermute | solution.py:46
  61.0 1.3 %shard_map.120 = (f32[32,8,128]{2,1,0:T(8,128)}, f32[1,2]{1,0:T(1,128)}) custom-call(s32[6]{0:T(128)S(1)} %stack.23.meta, f32[8,32,128]{2,1,0:T(8,128)S(1)} %get-tuple-element.64.whole, f32[72,128]{1,0:T(8,128)S(1)} %collective-permute-done.13.even_came, f32[72,128]{1,0:T(8,128)S(1)} %collective-permute-done.14.odd_came, f32[8,128]{1,0:T(8,128)S(1)} %add_add_fusion.squares), custom_call_target="tpu_custom_call" | custom-call | tf_op jit(solution)/shard_map/pallas_call | solution.py:54
  62.2 0.5 collective-permute-done.15
  62.8 0.5 slice.19
  (7 shorter events, 0.0 us)
Async XLA Ops:
  0.6 10.7 %collective-permute-start.3 = (bf16[96,128,128]{2,1,0:T(8,128)(2,1)}, bf16[96,128,128]{2,1,0:T(8,128)(2,1)S(1)}, u32[]{:S(2)}, u32[]{:S(2)}) collective-permute-start(bf16[96,128,128]{2,1,0:T(8,128)(2,1)} %bitcast.19), channel_id=1, source_target_pairs={{0,1},{1,0},{2,3},{3,2},{4,5},{5,4},{6,7},{7,6},{8,9},{9,8},{10,11... | collective-permute-start | bytes 9437192 | tf_op jit(solution)/shard_map/ppermute | solution.py:22
  5.0 3.2 %collective-permute-start.4 = (f32[16,32,128]{2,1,0:T(8,128)S(1)}, f32[16,32,128]{2,1,0:T(8,128)S(1)}, u32[]{:S(2)}, u32[]{:S(2)}) collective-permute-start(f32[16,32,128]{2,1,0:T(8,128)S(1)} %get-tuple-element.48), channel_id=1, source_target_pairs={{0,1},{1,0},{2,3},{3,2},{4,5},{5,4},{6,7},{7,6},{8,9},{9,8},{10,11... | collective-permute-start | bytes 786440 | tf_op jit(solution)/shard_map/ppermute | solution.py:22
  5.1 6.3 %collective-permute-start.2 = (bf16[4,32,128]{2,1,0:T(8,128)(2,1)S(1)}, bf16[4,32,128]{2,1,0:T(8,128)(2,1)S(1)}, u32[]{:S(2)}, u32[]{:S(2)}) collective-permute-start(bf16[4,32,128]{2,1,0:T(8,128)(2,1)S(1)} %get-tuple-element.46), channel_id=1, source_target_pairs={{0,2},{1,3},{2,0},{3,1},{4,6},{5,7},{6,4},{7,5},{8,10},{9,11},{10,... | collective-permute-start | bytes 98312 | tf_op jit(solution)/shard_map/ppermute | solution.py:22
  8.0 3.3 %collective-permute-start = (bf16[4,32,128]{2,1,0:T(8,128)(2,1)S(1)}, bf16[4,32,128]{2,1,0:T(8,128)(2,1)S(1)}, u32[]{:S(2)}, u32[]{:S(2)}) collective-permute-start(bf16[4,32,128]{2,1,0:T(8,128)(2,1)S(1)} %get-tuple-element.46), channel_id=1, source_target_pairs={{0,1},{1,0},{2,3},{3,2},{4,5},{5,4},{6,7},{7,6},{8,9},{9,8},{10,11... | collective-permute-start | bytes 98312 | tf_op jit(solution)/shard_map/ppermute | solution.py:22
  8.0 3.3 %collective-permute-start.1 = (bf16[4,32,128]{2,1,0:T(8,128)(2,1)S(1)}, bf16[4,32,128]{2,1,0:T(8,128)(2,1)S(1)}, u32[]{:S(2)}, u32[]{:S(2)}) collective-permute-start(bf16[4,32,128]{2,1,0:T(8,128)(2,1)S(1)} %get-tuple-element.45.rest_0_), channel_id=1, source_target_pairs={{0,3},{1,2},{2,1},{3,0},{4,7},{5,6},{6,5},{7,4},{8,11},{9,10},{10,... | collective-permute-start | bytes 98312 | tf_op jit(solution)/shard_map/ppermute | solution.py:22
  11.4 16.2 %copy-start = (s32[1,2,2]{2,1,0:T(2,128)S(1)}, s32[1,2,2]{2,1,0:T(2,128)}, u32[]{:S(2)}) copy-start(s32[1,2,2]{2,1,0:T(2,128)} %param.17) | copy-start | bytes 52
  22.4 5.2 %collective-permute-start.5 = (bf16[4,128,128]{2,1,0:T(8,128)(2,1)S(1)}, bf16[4,128,128]{2,1,0:T(8,128)(2,1)S(1)}, u32[]{:S(2)}, u32[]{:S(2)}) collective-permute-start(bf16[4,128,128]{2,1,0:T(8,128)(2,1)S(1)} %get-tuple-element.51), channel_id=1, source_target_pairs={{0,3},{1,2},{2,1},{3,0},{4,7},{5,6},{6,5},{7,4},{8,11},{9,10},{10,... | collective-permute-start | bytes 393224 | tf_op jit(solution)/shard_map/ppermute | solution.py:22
  23.0 3.3 %collective-permute-start.6 = (f32[2,32,128]{2,1,0:T(8,128)S(1)}, f32[2,32,128]{2,1,0:T(8,128)S(1)}, u32[]{:S(2)}, u32[]{:S(2)}) collective-permute-start(f32[2,32,128]{2,1,0:T(8,128)S(1)} %get-tuple-element.54), channel_id=1, source_target_pairs={{0,5},{1,4},{2,7},{3,6},{4,1},{5,0},{6,3},{7,2},{8,13},{9,12},{10,... | collective-permute-start | bytes 98312 | tf_op jit(solution)/shard_map/ppermute | solution.py:46
  24.6 1.7 %collective-permute-start.7 = (f32[2,32,128]{2,1,0:T(8,128)S(1)}, f32[2,32,128]{2,1,0:T(8,128)S(1)}, u32[]{:S(2)}, u32[]{:S(2)}) collective-permute-start(f32[2,32,128]{2,1,0:T(8,128)S(1)} %get-tuple-element.55), channel_id=1, source_target_pairs={{0,1},{1,0},{2,3},{3,2},{4,9},{5,8},{6,11},{7,10},{8,5},{9,4},{10,... | collective-permute-start | bytes 98312 | tf_op jit(solution)/shard_map/ppermute | solution.py:36
  28.3 12.5 %collective-permute-start.9 = (f32[4,96,128]{2,1,0:T(8,128)S(1)}, f32[4,96,128]{2,1,0:T(8,128)S(1)}, u32[]{:S(2)}, u32[]{:S(2)}) collective-permute-start(f32[4,96,128]{2,1,0:T(8,128)S(1)} %get-tuple-element.60), channel_id=1, source_target_pairs={{0,1},{1,0},{2,3},{3,2},{4,5},{5,4},{6,7},{7,6},{8,9},{9,8},{10,11... | collective-permute-start | bytes 589832 | tf_op jit(solution)/shard_map/ppermute | solution.py:22
  40.0 4.3 %collective-permute-start.8 = (bf16[4,64,128]{2,1,0:T(8,128)(2,1)S(1)}, bf16[4,64,128]{2,1,0:T(8,128)(2,1)S(1)}, u32[]{:S(2)}, u32[]{:S(2)}) collective-permute-start(bf16[4,64,128]{2,1,0:T(8,128)(2,1)S(1)} %get-tuple-element.58), channel_id=1, source_target_pairs={{0,3},{1,2},{2,1},{3,0},{4,7},{5,6},{6,5},{7,4},{8,11},{9,10},{10,... | collective-permute-start | bytes 196616 | tf_op jit(solution)/shard_map/ppermute | solution.py:22
  45.0 1.9 %collective-permute-start.10 = (f32[264,128]{1,0:T(8,128)S(1)}, f32[264,128]{1,0:T(8,128)S(1)}, u32[]{:S(2)}, u32[]{:S(2)}) collective-permute-start(f32[264,128]{1,0:T(8,128)S(1)} %get-tuple-element.63.packed), channel_id=1, source_target_pairs={{0,1},{1,0},{2,3},{3,2},{4,5},{5,4},{6,7},{7,6},{8,9},{9,8},{10,11... | collective-permute-start | bytes 405512 | tf_op jit(solution)/shard_map/ppermute | solution.py:22
  45.2 3.6 %collective-permute-start.12 = (f32[8,128]{1,0:T(8,128)S(1)}, f32[8,128]{1,0:T(8,128)S(1)}, u32[]{:S(2)}, u32[]{:S(2)}) collective-permute-start(f32[8,128]{1,0:T(8,128)S(1)} %get-tuple-element.67), channel_id=1, source_target_pairs={{0,2},{1,3},{2,0},{3,1},{4,6},{5,7},{6,4},{7,5},{8,10},{9,11},{10,... | collective-permute-start | bytes 12296 | tf_op jit(solution)/shard_map/ppermute | solution.py:22
  45.8 3.0 %collective-permute-start.11 = (f32[8,128]{1,0:T(8,128)S(1)}, f32[8,128]{1,0:T(8,128)S(1)}, u32[]{:S(2)}, u32[]{:S(2)}) collective-permute-start(f32[8,128]{1,0:T(8,128)S(1)} %get-tuple-element.67), channel_id=1, source_target_pairs={{0,3},{1,2},{2,1},{3,0},{4,7},{5,6},{6,5},{7,4},{8,11},{9,10},{10,... | collective-permute-start | bytes 12296 | tf_op jit(solution)/shard_map/ppermute | solution.py:22
  48.9 3.7 %collective-permute-start.13 = (f32[72,128]{1,0:T(8,128)S(1)}, f32[72,128]{1,0:T(8,128)S(1)}, u32[]{:S(2)}, u32[]{:S(2)}) collective-permute-start(f32[72,128]{1,0:T(8,128)S(1)} %pad_maximum_fusion), channel_id=1, source_target_pairs={{0,5},{1,4},{2,7},{3,6},{4,1},{5,0},{6,3},{7,2},{8,13},{9,12},{10,... | collective-permute-start | bytes 110600 | tf_op jit(solution)/shard_map/ppermute | solution.py:46
  52.6 6.3 %collective-permute-start.14 = (f32[72,128]{1,0:T(8,128)S(1)}, f32[72,128]{1,0:T(8,128)S(1)}, u32[]{:S(2)}, u32[]{:S(2)}) collective-permute-start(f32[72,128]{1,0:T(8,128)S(1)} %pad_maximum_fusion.1), channel_id=1, source_target_pairs={{0,29},{1,28},{2,31},{3,30},{4,9},{5,8},{6,11},{7,10},{8,5},{9,4},... | collective-permute-start | bytes 110600 | tf_op jit(solution)/shard_map/ppermute | solution.py:36
  58.9 3.9 %collective-permute-start.15 = (f32[8,128]{1,0:T(8,128)S(1)}, f32[8,128]{1,0:T(8,128)S(1)}, u32[]{:S(2)}, u32[]{:S(2)}) collective-permute-start(f32[8,128]{1,0:T(8,128)S(1)} %slice_add_fusion), channel_id=1, source_target_pairs={{0,17},{1,16},{2,19},{3,18},{4,21},{5,20},{6,23},{7,22},{8,25},{9,... | collective-permute-start | bytes 12296 | tf_op jit(solution)/shard_map/ppermute | solution.py:46

commit v2 on v1

--- a/solution.py
+++ b/solution.py
@@ -36,10 +36,20 @@
     return lax.ppermute(value, ("frag", "blk"), links)
 
 
-def wide_swap(value, frag_step):
+def odd_far_swap(value):
+    count, width = lax.axis_size("frag"), lax.axis_size("blk")
+    links = []
+    for f in range(count):
+        source = f ^ 4
+        source = (source + (1 if source % 2 else -1)) % count
+        links += [(source * width + (b ^ 1), f * width + b) for b in range(width)]
+    return lax.ppermute(value, ("frag", "blk"), links)
+
+
+def wide_swap(value, frag_step, blk_step=1):
     count = lax.axis_size("blk")
     links = [
-        (f * count + b, (f ^ frag_step) * count + (b ^ 1))
+        (f * count + b, (f ^ frag_step) * count + (b ^ blk_step))
         for f in range(lax.axis_size("frag"))
         for b in range(count)
     ]
@@ -187,7 +197,25 @@
     fock_low[1] = (scaled - high.astype(F32)).astype(BF16)
 
 
-def hole_body(meta, occ, pair, amp, from_mate, keep, came, fock, level, base):
+def hole_body(
+    meta,
+    occ,
+    pair,
+    picked,
+    amp,
+    from_mate,
+    keep,
+    came,
+    fock,
+    level,
+    own,
+    even_came,
+    odd_came,
+    base,
+    keep_weights,
+    mate_weights,
+    weights,
+):
     half_count, rows, virt = amp.shape
     core, chip, half = meta[0], meta[1], meta[2]
     turned = times_fock(amp[...].reshape(half_count * rows, virt), fock[...])
@@ -198,8 +226,20 @@
         total = total + turned[p * rows : (p + 1) * rows] - (levels - pair[0, at]) * amp[p]
         for r in range(half_count):
             total = total + occ[at, half * half_count + r] * amp[r]
-            total = total + occ[at, (1 - half) * half_count + r] * from_mate[r, :rows, :]
+            total = total + occ[at, (1 - half) * half_count + r] * from_mate[r]
         base[p] = total
+    is_even, at_start, at_end = meta[3] % 2 == 0, meta[3] == 0, meta[3] == meta[4]
+    weights[...] = own[...]
+    for r in range(even_came.shape[0]):
+        above = jnp.where(is_even, even_came[r], odd_came[r])
+        below = jnp.where(is_even, odd_came[r], even_came[r])
+        at = picked[0, r]
+        weights[at] = weights[at] + jnp.where(at_end, 0.0, above)
+        at = picked[1, r]
+        weights[at] = weights[at] + jnp.where(at_start, 0.0, below)
+    for p in range(half_count):
+        keep_weights[p] = weights[half * half_count + p]
+        mate_weights[p] = weights[(1 - half) * half_count + p]
 
 
 def ladder_body(meta, fock_low, *rest, group, count):
@@ -323,21 +363,14 @@
 def middle_body(
     meta,
     pair,
-    picked,
     part,
     part_came,
     level,
     keep,
     came,
-    own,
-    even_came,
-    odd_came,
     amp,
     low,
     squares,
-    to_mate,
-    keep_weights,
-    weights,
 ):
     half_count, rows, _ = amp.shape
     core, chip, half = meta[0], meta[1], meta[2]
@@ -350,27 +383,14 @@
         fresh = (join(core == 0, keep[2 * half_count + p], came[2 * half_count + p]) + lad) / (level[mine, :] - shift_by)
         norm = norm + fold_squares(join(core == 0, keep[half_count + p], came[half_count + p]) + lad)
         amp[p] = fresh
-        to_mate[p, :rows, :] = fresh
         low[p, mine, :] = fresh.astype(BF16)
         total = part[p, other, :] + part_came[p, other, :].astype(F32)
         low[p, other, :] = (total / (level[other, :] - shift_by)).astype(BF16)
     squares[...] = norm
-    is_even, at_start, at_end = meta[3] % 2 == 0, meta[3] == 0, meta[3] == meta[4]
-    weights[...] = own[...]
-    for r in range(even_came.shape[0]):
-        above = jnp.where(is_even, even_came[r], odd_came[r])
-        below = jnp.where(is_even, odd_came[r], even_came[r])
-        at = picked[0, r]
-        weights[at] = weights[at] + jnp.where(at_end, 0.0, above)
-        at = picked[1, r]
-        weights[at] = weights[at] + jnp.where(at_start, 0.0, below)
-    for p in range(half_count):
-        keep_weights[p] = weights[half * half_count + p]
-        to_mate[p, rows:, :] = weights[(1 - half) * half_count + p]
 
 
 def last_body(
-    meta, pair, part, came, level, base, amp, keep_weights, from_mate, first, packed, sums_out
+    meta, pair, part, came, level, base, amp, keep_weights, from_mate, first, packed
 ):
     half_count, rows, virt = base.shape
     core, chip, half = meta[0], meta[1], meta[2]
@@ -385,15 +405,14 @@
         top, bottom = fresh[:single], fresh[single:]
         mine = jnp.where(core == 0, top, bottom)
         mate = jnp.where(core == 0, bottom, top)
-        energy = energy + keep_weights[p] * mine + from_mate[p, rows:, :] * mate
+        energy = energy + keep_weights[p] * mine + from_mate[p] * mate
         packed[p * single : (p + 1) * single, :] = mine
         packed[(half_count + p) * single : (half_count + p + 1) * single, :] = mate
-    slot = lax.broadcasted_iota(jnp.int32, sums_out.shape, 0)
+    slot = lax.broadcasted_iota(jnp.int32, first.shape, 0)
     sums = jnp.where(slot == 0, jnp.sum(energy), 0.0)
     sums = jnp.where(slot == 1, jnp.sum(first[...]), sums)
     sums = jnp.where(slot == 2, jnp.sum(norm), sums)
     packed[2 * half_count * single :, :] = sums
-    sums_out[...] = sums
 
 
 def border_body(meta, picked, packed, came, whole, even_rows, odd_rows, sums, mate):
@@ -521,43 +540,44 @@
     odd_came = odd_swap(odd_weights, False)
     small = shaped(8, virt)
     low = shaped(half_count, virt, virt, dtype=BF16)
-    amp, low, first, to_mate, keep_weights = call(
+    amp, low, first = call(
         middle_body,
-        (own, low, small, shaped(half_count, both + row_count, virt), single),
-        (SMEM, SMEM, SMEM) + (VMEM,) * 8,
+        (own, low, small),
+        (SMEM, SMEM) + (VMEM,) * 5,
         meta,
         pair,
-        export_rows[0],
         part,
         part_came,
         level,
         keep,
         came,
+    )
+    mate_amp = swap(amp, 1)
+    send, part = ladder(meta, fock_low, (low,), near, far)
+    part_came = swap(send, CROSS)
+    base, keep_weights, mate_weights = call(
+        hole_body,
+        (own, single, single),
+        (SMEM,) * 4 + (VMEM,) * 9,
+        meta,
+        occ,
+        pair,
+        export_rows[0],
+        amp,
+        mate_amp,
+        keep,
+        came,
+        fock,
+        level,
         own_weights,
         even_came,
         odd_came,
         scratch=(pltpu.VMEM((pairs, row_count, virt), F32),),
     )
-    from_mate = swap(to_mate, 1)
-    send, part = ladder(meta, fock_low, (low,), near, far)
-    part_came = swap(send, CROSS)
-    base = call(
-        hole_body,
-        own,
-        (SMEM, SMEM, SMEM) + (VMEM,) * 6,
-        meta,
-        occ,
-        pair,
-        amp,
-        from_mate,
-        keep,
-        came,
-        fock,
-        level,
-    )
-    packed, sums = call(
+    from_mate = swap(mate_weights, 1)
+    packed = call(
         last_body,
-        (shaped(pairs * row_count + 8, virt), small),
+        shaped(pairs * row_count + 8, virt),
         (SMEM, SMEM) + (VMEM,) * 8,
         meta,
         pair,
@@ -571,8 +591,6 @@
         first,
     )
     last_came = swap(packed, 1)
-    sum_cross = swap(sums, CROSS)
-    sum_diag = swap(sums, CROSS ^ 1)
     rows = shaped(border * row_count, virt)
     whole, even_rows, odd_rows, sums = call(
         border_body,
@@ -584,13 +602,20 @@
         last_came,
         scratch=(pltpu.VMEM((pairs, row_count, virt), F32),),
     )
-    sums = sums + (sum_cross + sum_diag)
-    norm_squares = sums
+    tail = border * row_count
     even_came = even_swap(jnp.concatenate([even_rows, sums], axis=0))
-    sums = sums + even_came[border * row_count :]
+    cross = swap(sums, CROSS)
+    both_came = wide_swap(sums, 1, CROSS)
+    norm_squares = sums + cross
+    sums = norm_squares + (even_came[tail:] + both_came)
     odd_came = odd_swap(jnp.concatenate([odd_rows, sums], axis=0), True)
-    sums = sums + odd_came[border * row_count :]
-    step = 4
+    if lax.axis_size("frag") > 4:
+        far_came = wide_swap(sums, 4)
+        next_came = odd_far_swap(sums)
+        sums = (sums + odd_came[tail:]) + (far_came + next_came)
+    else:
+        sums = sums + odd_came[tail:]
+    step = 8
     while step < lax.axis_size("frag"):
         sums = sums + wide_swap(sums, step)
         step *= 2

time: 65.3 us -> 64.1 us (0.982)
  starting transfers between devices: 18.1 us -> 15.9 us
  waiting for transfers between devices: 13.8 us -> 14.8 us
    ppermute x0 -> x1, waiting for transfers between devices: none -> 3.04 us  [odd_far_swap(): return lax.ppermute(value, ('frag', 'blk'), links)]
    ppermute x2, waiting for transfers between devices: 1.65 us -> 0.01 us  [odd_swap(): return lax.ppermute(value, ('frag', 'blk'), links)]
    ppermute x3 -> x4, starting transfers between devices: 5.75 us -> 4.21 us  [wide_swap(): return lax.ppermute(value, ('frag', 'blk'), links)]
    ppermute x3 -> x4, waiting for transfers between devices: 3.75 us -> 2.25 us  [wide_swap(): return lax.ppermute(value, ('frag', 'blk'), links)]
    ppermute x11, waiting for transfers between devices: 8.42 us -> 9.55 us  [swap(): return lax.ppermute(value, 'blk', [(at, at ^ step) for at in range(count)])]
  transfers between devices with their start and end apart: 16 -> 18, of which waited for: 9 -> 6; matrix products, arithmetic and copies ran while one was open for 0% -> 0% of each run, Pallas kernels for 27% -> 26%
where the time goes in v2:
time: 64.1 us; the launch traced here: 64 us
  Pallas kernels  30.1 us (47%)
  starting transfers between devices  15.9 us (25%)
  waiting for transfers between devices  14.8 us (23%)
  between operations  2.53 us (4%)
    pallas_call x9, Pallas kernels, call(): pl.pallas_call(body, out_shape=out_shape, in_specs=specs, out_specs=jax.t...  30.1 us
    ppermute x11, waiting for transfers between devices, swap(): return lax.ppermute(value, 'blk', [(at, at ^ step) for at in range(count)])  9.55 us
    ppermute x11, starting transfers between devices, swap(): return lax.ppermute(value, 'blk', [(at, at ^ step) for at in range(count)])  7.36 us
    ppermute x2, starting transfers between devices, odd_swap(): return lax.ppermute(value, ('frag', 'blk'), links)  4.33 us
    ppermute x4, starting transfers between devices, wide_swap(): return lax.ppermute(value, ('frag', 'blk'), links)  4.21 us
    ppermute x1, waiting for transfers between devices, odd_far_swap(): return lax.ppermute(value, ('frag', 'blk'), links)  3.04 us
    ppermute x4, waiting for transfers between devices, wide_swap(): return lax.ppermute(value, ('frag', 'blk'), links)  2.25 us
  transfers between devices with their start and end apart: 18, of which 6 were waited for; matrix products, arithmetic and copies ran while one was open for 0% of the time, Pallas kernels for 26%

profile of v2, /device:TPU:0, one launch (start us, length us, event | category | flops | bytes accessed | tf_op | source)
XLA Modules:
  0.0 64.0 jit_solution(17843189594203284865)
XLA Ops:
  0.6 0.6 collective-permute-start.3
  1.2 0.1 stack.23.meta
  1.3 1.7 %shard_map.112 = (bf16[4,32,128]{2,1,0:T(8,128)(2,1)S(1)}, bf16[4,32,128]{2,1,0:T(8,128)(2,1)S(1)}, f32[32,8,128]{2,1,0:T(8,128)S(1)}, f32[32,8,128]{2,1,0:T(8,1...) custom-call(s32[6]{0:T(128)S(1)} %stack.23.meta, ...), custom_call_target="tpu_custom_call" | custom-call | tf_op jit(solution)/shard_map/pallas_call | solution.py:64
  3.0 2.0 %shard_map.113 = (f32[12,32,128]{2,1,0:T(8,128)S(1)}, f32[16,32,128]{2,1,0:T(8,128)S(1)}, f32[128,128]{1,0:T(8,128)S(1)}, bf16[2,128,128]{2,1,0:T(8,128)(2,1)S(1)}, f32[8,32,128]{2,1,0:T(8,128)S(1)}) custom-call(s32[6]{0:T(128)S(1)} %stack.23.meta, f32[8,8]{1,0:T(8,128)S(1)} %get-tuple-element.37.occ, f32[1,8]{1,0:T(1,128)S(1)} %get-tuple-element.36.pair, ...), custom_call_target="tpu_custom_call" | custom-call | tf_op jit(solution)/shard_map/pallas_call | solution.py:64
  5.0 0.1 collective-permute-start.4
  5.1 2.9 %collective-permute-start.2 = (bf16[4,32,128]{2,1,0:T(8,128)(2,1)S(1)}, bf16[4,32,128]{2,1,0:T(8,128)(2,1)S(1)}, u32[]{:S(2)}, u32[]{:S(2)}) collective-permute-start(bf16[4,32,128]{2,1,0:T(8,128)(2,1)S(1)} %get-tuple-element.45), channel_id=1, source_target_pairs={{0,2},{1,3},{2,0},{3,1},{4,6},{5,7},{6,4},{7,5},{8,10},{9,11},{10,... | collective-permute-start | bytes 98312 | tf_op jit(solution)/shard_map/ppermute | solution.py:22
  8.0 0.0 collective-permute-start
  8.0 0.1 collective-permute-start.1
  8.1 0.0 collective-permute-done.4.rest_7_.came
  8.1 3.2 %collective-permute-done.1.rest_2_ = bf16[4,32,128]{2,1,0:T(8,128)(2,1)S(1)} collective-permute-done((bf16[4,32,128]{2,1,0:T(8,128)(2,1)S(1)}, bf16[4,32,128]{2,1,0:T(8,128)(2,1)S(1)}, u32[]{:S(2)}, u32[]{:S(2)}) %collective-permute-start.1) | collective-permute-done | bytes 32800 | tf_op jit(solution)/shard_map/ppermute | solution.py:22
  11.3 0.0 collective-permute-done.2.rest_3_
  11.3 0.0 collective-permute-done.rest_1_
  11.4 0.0 collective-permute-done.3.rest_5_.rest_2_
  11.4 11.0 %shard_map.114 = (f32[4,128,128]{2,1,0:T(8,128)S(1)}, bf16[4,128,128]{2,1,0:T(8,128)(2,1)S(1)}) custom-call(s32[6]{0:T(128)S(1)} %stack.23.meta, bf16[2,128,128]{2,1,0:T(8,128)(2,1)S(1)} %get-tuple-element.43.fock_low, bf16[4,32,128]{2,1,0:T(8,128)(2,1)S(1)} %get-tuple-element.44.rest_0_, bf16[4,32,128]{2,1,0:T(8,128)(2,1)S(1)} %collective-permute-done.rest_1_, ...), custom_call_target="tpu_custom_call" | custom-call | flops 6442450944 | tf_op jit(solution)/shard_map/pallas_call | solution.py:64
  22.4 0.6 collective-permute-start.5
  23.0 1.6 %collective-permute-start.8 = (f32[2,32,128]{2,1,0:T(8,128)S(1)}, f32[2,32,128]{2,1,0:T(8,128)S(1)}, u32[]{:S(2)}, u32[]{:S(2)}) collective-permute-start(f32[2,32,128]{2,1,0:T(8,128)S(1)} %get-tuple-element.57), channel_id=1, source_target_pairs={{0,5},{1,4},{2,7},{3,6},{4,1},{5,0},{6,3},{7,2},{8,13},{9,12},{10,... | collective-permute-start | bytes 98312 | tf_op jit(solution)/shard_map/ppermute | solution.py:56
  24.6 0.2 collective-permute-start.9
  24.8 2.8 %collective-permute-done.5.part_came = bf16[4,128,128]{2,1,0:T(8,128)(2,1)S(1)} collective-permute-done((bf16[4,128,128]{2,1,0:T(8,128)(2,1)S(1)}, bf16[4,128,128]{2,1,0:T(8,128)(2,1)S(1)}, u32[]{:S(2)}, u32[]{:S(2)}) %collective-permute-start.5) | collective-permute-done | bytes 131104 | tf_op jit(solution)/shard_map/ppermute | solution.py:22
  27.6 0.6 shard_map.115
  28.2 0.6 collective-permute-start.7
  28.8 11.2 %shard_map.116 = (bf16[4,64,128]{2,1,0:T(8,128)(2,1)S(1)}, f32[4,64,128]{2,1,0:T(8,128)S(1)}) custom-call(s32[6]{0:T(128)S(1)} %stack.23.meta, bf16[2,128,128]{2,1,0:T(8,128)(2,1)S(1)} %get-tuple-element.43.fock_low, bf16[4,128,128]{2,1,0:T(8,128)(2,1)S(1)} %get-tuple-element.52.rest_0_, bf16[96,128,128]{2,1,0:T(8,128)(2,1)} %bitcast.21, ...), custom_call_target="tpu_custom_call" | custom-call | flops 6442450944 | tf_op jit(solution)/shard_map/pallas_call | solution.py:64
  40.0 0.7 %collective-permute-start.6 = (bf16[4,64,128]{2,1,0:T(8,128)(2,1)S(1)}, bf16[4,64,128]{2,1,0:T(8,128)(2,1)S(1)}, u32[]{:S(2)}, u32[]{:S(2)}) collective-permute-start(bf16[4,64,128]{2,1,0:T(8,128)(2,1)S(1)} %get-tuple-element.54), channel_id=1, source_target_pairs={{0,3},{1,2},{2,1},{3,0},{4,7},{5,6},{6,5},{7,4},{8,11},{9,10},{10,... | collective-permute-start | bytes 196616 | tf_op jit(solution)/shard_map/ppermute | solution.py:22
  40.7 0.0 collective-permute-done.8.even_came
  40.7 0.0 collective-permute-done.9.odd_came
  40.7 0.0 collective-permute-done.7.from_mate
  40.7 0.0 copy-done
  40.8 1.0 %shard_map.117 = (f32[4,64,128]{2,1,0:T(8,128)S(1)}, f32[4,32,128]{2,1,0:T(8,128)S(1)}, f32[4,32,128]{2,1,0:T(8,128)S(1)}) custom-call(s32[6]{0:T(128)S(1)} %stack.23.meta, f32[8,8]{1,0:T(8,128)S(1)} %get-tuple-element.37.occ, f32[1,8]{1,0:T(1,128)S(1)} %get-tuple-element.36.pair, s32[2,2]{1,0:T(2,128)S(1)} %bitcast.13, ...), custom_call_target="tpu_custom_call" | custom-call | tf_op jit(solution)/shard_map/pallas_call | solution.py:64
  41.7 0.2 collective-permute-start.10
  42.0 2.3 %collective-permute-done.6.came = bf16[4,64,128]{2,1,0:T(8,128)(2,1)S(1)} collective-permute-done((bf16[4,64,128]{2,1,0:T(8,128)(2,1)S(1)}, bf16[4,64,128]{2,1,0:T(8,128)(2,1)S(1)}, u32[]{:S(2)}, u32[]{:S(2)}) %collective-permute-start.6) | collective-permute-done | bytes 65568 | tf_op jit(solution)/shard_map/ppermute | solution.py:22
  44.2 0.0 collective-permute-done.10.from_mate
  44.2 0.7 %shard_map.118.packed = f32[264,128]{1,0:T(8,128)S(1)} custom-call(s32[6]{0:T(128)S(1)} %stack.23.meta, f32[1,8]{1,0:T(1,128)S(1)} %get-tuple-element.36.pair, f32[4,64,128]{2,1,0:T(8,128)S(1)} %get-tuple-element.53.part, bf16[4,64,128]{2,1,0:T(8,128)(2,1)S(1)} %collective-permute-done.6.came, f32[128,128]{1,0:T(8,128)S(1)} %get-tuple-element.51.level, ...), custom_call_target="tpu_custom_call" | custom-call | tf_op jit(solution)/shard_map/pallas_call | solution.py:64
  45.0 0.2 collective-permute-start.11
  45.2 1.2 %collective-permute-done.11.came = f32[264,128]{1,0:T(8,128)S(1)} collective-permute-done((f32[264,128]{1,0:T(8,128)S(1)}, f32[264,128]{1,0:T(8,128)S(1)}, u32[]{:S(2)}, u32[]{:S(2)}) %collective-permute-start.11) | collective-permute-done | bytes 135200 | tf_op jit(solution)/shard_map/ppermute | solution.py:22
  46.4 0.6 shard_map.119
  47.0 1.3 %collective-permute-start.12 = (f32[72,128]{1,0:T(8,128)S(1)}, f32[72,128]{1,0:T(8,128)S(1)}, u32[]{:S(2)}, u32[]{:S(2)}) collective-permute-start(f32[72,128]{1,0:T(8,128)S(1)} %pad_maximum_fusion), channel_id=1, source_target_pairs={{0,5},{1,4},{2,7},{3,6},{4,1},{5,0},{6,3},{7,2},{8,13},{9,12},{10,... | collective-permute-start | bytes 110600 | tf_op jit(solution)/shard_map/ppermute | solution.py:56
  48.3 0.4 collective-permute-start.14
  48.7 1.3 %collective-permute-start.13 = (f32[8,128]{1,0:T(8,128)S(1)}, f32[8,128]{1,0:T(8,128)S(1)}, u32[]{:S(2)}, u32[]{:S(2)}) collective-permute-start(f32[8,128]{1,0:T(8,128)S(1)} %get-tuple-element.65), channel_id=1, source_target_pairs={{0,3},{1,2},{2,1},{3,0},{4,7},{5,6},{6,5},{7,4},{8,11},{9,10},{10,... | collective-permute-start | bytes 12296 | tf_op jit(solution)/shard_map/ppermute | solution.py:22
  50.0 2.2 %collective-permute-done.14 = f32[8,128]{1,0:T(8,128)S(1)} collective-permute-done((f32[8,128]{1,0:T(8,128)S(1)}, f32[8,128]{1,0:T(8,128)S(1)}, u32[]{:S(2)}, u32[]{:S(2)}) %collective-permute-start.14) | collective-permute-done | bytes 4128 | tf_op jit(solution)/shard_map/ppermute | solution.py:56
  52.3 0.0 collective-permute-done.13
  52.3 0.0 collective-permute-done.12.even_came
  52.3 4.1 %collective-permute-start.15 = (f32[72,128]{1,0:T(8,128)S(1)}, f32[72,128]{1,0:T(8,128)S(1)}, u32[]{:S(2)}, u32[]{:S(2)}) collective-permute-start(f32[72,128]{1,0:T(8,128)S(1)} %pad_maximum_fusion.1), channel_id=1, source_target_pairs={{0,29},{1,28},{2,31},{3,30},{4,9},{5,8},{6,11},{7,10},{8,5},{9,4},... | collective-permute-start | bytes 110600 | tf_op jit(solution)/shard_map/ppermute | solution.py:36
  56.4 0.0 collective-permute-start.17
  56.4 0.9 %collective-permute-start.16 = (f32[8,128]{1,0:T(8,128)S(1)}, f32[8,128]{1,0:T(8,128)S(1)}, u32[]{:S(2)}, u32[]{:S(2)}) collective-permute-start(f32[8,128]{1,0:T(8,128)S(1)} %get-tuple-element.69), channel_id=1, source_target_pairs={{0,17},{1,16},{2,19},{3,18},{4,21},{5,20},{6,23},{7,22},{8,25},{9,... | collective-permute-start | bytes 12296 | tf_op jit(solution)/shard_map/ppermute | solution.py:56
  57.3 3.0 %collective-permute-done.17 = f32[8,128]{1,0:T(8,128)S(1)} collective-permute-done((f32[8,128]{1,0:T(8,128)S(1)}, f32[8,128]{1,0:T(8,128)S(1)}, u32[]{:S(2)}, u32[]{:S(2)}) %collective-permute-start.17) | collective-permute-done | bytes 4128 | tf_op jit(solution)/shard_map/ppermute | solution.py:46
  60.4 0.0 collective-permute-done.16
  60.4 0.0 collective-permute-done.15.odd_came
  60.4 0.5 slice.19
  61.6 1.3 %shard_map.120 = (f32[32,8,128]{2,1,0:T(8,128)}, f32[1,2]{1,0:T(1,128)}) custom-call(s32[6]{0:T(128)S(1)} %stack.23.meta, f32[8,32,128]{2,1,0:T(8,128)S(1)} %get-tuple-element.63.whole, f32[72,128]{1,0:T(8,128)S(1)} %collective-permute-done.12.even_came, f32[72,128]{1,0:T(8,128)S(1)} %collective-permute-done.15.odd_came, f32[8,128]{1,0:T(8,128)S(1)} %get-tuple-element.70.squares), custom_call_target="tpu_custom_call" | custom-call | tf_op jit(solution)/shard_map/pallas_call | solution.py:64
  (6 shorter events, 0.0 us)
Async XLA Ops:
  0.6 10.7 %collective-permute-start.3 = (bf16[96,128,128]{2,1,0:T(8,128)(2,1)}, bf16[96,128,128]{2,1,0:T(8,128)(2,1)S(1)}, u32[]{:S(2)}, u32[]{:S(2)}) collective-permute-start(bf16[96,128,128]{2,1,0:T(8,128)(2,1)} %bitcast.19), channel_id=1, source_target_pairs={{0,1},{1,0},{2,3},{3,2},{4,5},{5,4},{6,7},{7,6},{8,9},{9,8},{10,11... | collective-permute-start | bytes 9437192 | tf_op jit(solution)/shard_map/ppermute | solution.py:22
  5.0 3.2 %collective-permute-start.4 = (f32[16,32,128]{2,1,0:T(8,128)S(1)}, f32[16,32,128]{2,1,0:T(8,128)S(1)}, u32[]{:S(2)}, u32[]{:S(2)}) collective-permute-start(f32[16,32,128]{2,1,0:T(8,128)S(1)} %get-tuple-element.47), channel_id=1, source_target_pairs={{0,1},{1,0},{2,3},{3,2},{4,5},{5,4},{6,7},{7,6},{8,9},{9,8},{10,11... | collective-permute-start | bytes 786440 | tf_op jit(solution)/shard_map/ppermute | solution.py:22
  5.1 6.3 %collective-permute-start.2 = (bf16[4,32,128]{2,1,0:T(8,128)(2,1)S(1)}, bf16[4,32,128]{2,1,0:T(8,128)(2,1)S(1)}, u32[]{:S(2)}, u32[]{:S(2)}) collective-permute-start(bf16[4,32,128]{2,1,0:T(8,128)(2,1)S(1)} %get-tuple-element.45), channel_id=1, source_target_pairs={{0,2},{1,3},{2,0},{3,1},{4,6},{5,7},{6,4},{7,5},{8,10},{9,11},{10,... | collective-permute-start | bytes 98312 | tf_op jit(solution)/shard_map/ppermute | solution.py:22
  8.0 3.3 %collective-permute-start = (bf16[4,32,128]{2,1,0:T(8,128)(2,1)S(1)}, bf16[4,32,128]{2,1,0:T(8,128)(2,1)S(1)}, u32[]{:S(2)}, u32[]{:S(2)}) collective-permute-start(bf16[4,32,128]{2,1,0:T(8,128)(2,1)S(1)} %get-tuple-element.45), channel_id=1, source_target_pairs={{0,1},{1,0},{2,3},{3,2},{4,5},{5,4},{6,7},{7,6},{8,9},{9,8},{10,11... | collective-permute-start | bytes 98312 | tf_op jit(solution)/shard_map/ppermute | solution.py:22
  8.0 3.3 %collective-permute-start.1 = (bf16[4,32,128]{2,1,0:T(8,128)(2,1)S(1)}, bf16[4,32,128]{2,1,0:T(8,128)(2,1)S(1)}, u32[]{:S(2)}, u32[]{:S(2)}) collective-permute-start(bf16[4,32,128]{2,1,0:T(8,128)(2,1)S(1)} %get-tuple-element.44.rest_0_), channel_id=1, source_target_pairs={{0,3},{1,2},{2,1},{3,0},{4,7},{5,6},{6,5},{7,4},{8,11},{9,10},{10,... | collective-permute-start | bytes 98312 | tf_op jit(solution)/shard_map/ppermute | solution.py:22
  22.4 5.2 %collective-permute-start.5 = (bf16[4,128,128]{2,1,0:T(8,128)(2,1)S(1)}, bf16[4,128,128]{2,1,0:T(8,128)(2,1)S(1)}, u32[]{:S(2)}, u32[]{:S(2)}) collective-permute-start(bf16[4,128,128]{2,1,0:T(8,128)(2,1)S(1)} %get-tuple-element.50), channel_id=1, source_target_pairs={{0,3},{1,2},{2,1},{3,0},{4,7},{5,6},{6,5},{7,4},{8,11},{9,10},{10,... | collective-permute-start | bytes 393224 | tf_op jit(solution)/shard_map/ppermute | solution.py:22
  23.0 17.7 %collective-permute-start.8 = (f32[2,32,128]{2,1,0:T(8,128)S(1)}, f32[2,32,128]{2,1,0:T(8,128)S(1)}, u32[]{:S(2)}, u32[]{:S(2)}) collective-permute-start(f32[2,32,128]{2,1,0:T(8,128)S(1)} %get-tuple-element.57), channel_id=1, source_target_pairs={{0,5},{1,4},{2,7},{3,6},{4,1},{5,0},{6,3},{7,2},{8,13},{9,12},{10,... | collective-permute-start | bytes 98312 | tf_op jit(solution)/shard_map/ppermute | solution.py:56
  24.6 16.2 %collective-permute-start.9 = (f32[2,32,128]{2,1,0:T(8,128)S(1)}, f32[2,32,128]{2,1,0:T(8,128)S(1)}, u32[]{:S(2)}, u32[]{:S(2)}) collective-permute-start(f32[2,32,128]{2,1,0:T(8,128)S(1)} %get-tuple-element.58), channel_id=1, source_target_pairs={{0,1},{1,0},{2,3},{3,2},{4,9},{5,8},{6,11},{7,10},{8,5},{9,4},{10,... | collective-permute-start | bytes 98312 | tf_op jit(solution)/shard_map/ppermute | solution.py:36
  28.2 12.5 %collective-permute-start.7 = (f32[4,64,128]{2,1,0:T(8,128)S(1)}, f32[4,64,128]{2,1,0:T(8,128)S(1)}, u32[]{:S(2)}, u32[]{:S(2)}) collective-permute-start(f32[4,64,128]{2,1,0:T(8,128)S(1)} %get-tuple-element.55.amp), channel_id=1, source_target_pairs={{0,1},{1,0},{2,3},{3,2},{4,5},{5,4},{6,7},{7,6},{8,9},{9,8},{10,11... | collective-permute-start | bytes 393224 | tf_op jit(solution)/shard_map/ppermute | solution.py:22
  28.8 12.0 %copy-start = (s32[1,2,2]{2,1,0:T(2,128)S(1)}, s32[1,2,2]{2,1,0:T(2,128)}, u32[]{:S(2)}) copy-start(s32[1,2,2]{2,1,0:T(2,128)} %param.17) | copy-start | bytes 52
  40.0 4.2 %collective-permute-start.6 = (bf16[4,64,128]{2,1,0:T(8,128)(2,1)S(1)}, bf16[4,64,128]{2,1,0:T(8,128)(2,1)S(1)}, u32[]{:S(2)}, u32[]{:S(2)}) collective-permute-start(bf16[4,64,128]{2,1,0:T(8,128)(2,1)S(1)} %get-tuple-element.54), channel_id=1, source_target_pairs={{0,3},{1,2},{2,1},{3,0},{4,7},{5,6},{6,5},{7,4},{8,11},{9,10},{10,... | collective-permute-start | bytes 196616 | tf_op jit(solution)/shard_map/ppermute | solution.py:22
  41.7 2.5 %collective-permute-start.10 = (f32[4,32,128]{2,1,0:T(8,128)S(1)}, f32[4,32,128]{2,1,0:T(8,128)S(1)}, u32[]{:S(2)}, u32[]{:S(2)}) collective-permute-start(f32[4,32,128]{2,1,0:T(8,128)S(1)} %get-tuple-element.61), channel_id=1, source_target_pairs={{0,1},{1,0},{2,3},{3,2},{4,5},{5,4},{6,7},{7,6},{8,9},{9,8},{10,11... | collective-permute-start | bytes 196616 | tf_op jit(solution)/shard_map/ppermute | solution.py:22
  45.0 1.4 %collective-permute-start.11 = (f32[264,128]{1,0:T(8,128)S(1)}, f32[264,128]{1,0:T(8,128)S(1)}, u32[]{:S(2)}, u32[]{:S(2)}) collective-permute-start(f32[264,128]{1,0:T(8,128)S(1)} %shard_map.118.packed), channel_id=1, source_target_pairs={{0,1},{1,0},{2,3},{3,2},{4,5},{5,4},{6,7},{7,6},{8,9},{9,8},{10,11... | collective-permute-start | bytes 405512 | tf_op jit(solution)/shard_map/ppermute | solution.py:22
  47.0 5.3 %collective-permute-start.12 = (f32[72,128]{1,0:T(8,128)S(1)}, f32[72,128]{1,0:T(8,128)S(1)}, u32[]{:S(2)}, u32[]{:S(2)}) collective-permute-start(f32[72,128]{1,0:T(8,128)S(1)} %pad_maximum_fusion), channel_id=1, source_target_pairs={{0,5},{1,4},{2,7},{3,6},{4,1},{5,0},{6,3},{7,2},{8,13},{9,12},{10,... | collective-permute-start | bytes 110600 | tf_op jit(solution)/shard_map/ppermute | solution.py:56
  48.3 3.9 %collective-permute-start.14 = (f32[8,128]{1,0:T(8,128)S(1)}, f32[8,128]{1,0:T(8,128)S(1)}, u32[]{:S(2)}, u32[]{:S(2)}) collective-permute-start(f32[8,128]{1,0:T(8,128)S(1)} %get-tuple-element.65), channel_id=1, source_target_pairs={{0,7},{1,6},{2,5},{3,4},{4,3},{5,2},{6,1},{7,0},{8,15},{9,14},{10,... | collective-permute-start | bytes 12296 | tf_op jit(solution)/shard_map/ppermute | solution.py:56
  48.7 3.5 %collective-permute-start.13 = (f32[8,128]{1,0:T(8,128)S(1)}, f32[8,128]{1,0:T(8,128)S(1)}, u32[]{:S(2)}, u32[]{:S(2)}) collective-permute-start(f32[8,128]{1,0:T(8,128)S(1)} %get-tuple-element.65), channel_id=1, source_target_pairs={{0,3},{1,2},{2,1},{3,0},{4,7},{5,6},{6,5},{7,4},{8,11},{9,10},{10,... | collective-permute-start | bytes 12296 | tf_op jit(solution)/shard_map/ppermute | solution.py:22
  52.3 8.1 %collective-permute-start.15 = (f32[72,128]{1,0:T(8,128)S(1)}, f32[72,128]{1,0:T(8,128)S(1)}, u32[]{:S(2)}, u32[]{:S(2)}) collective-permute-start(f32[72,128]{1,0:T(8,128)S(1)} %pad_maximum_fusion.1), channel_id=1, source_target_pairs={{0,29},{1,28},{2,31},{3,30},{4,9},{5,8},{6,11},{7,10},{8,5},{9,4},... | collective-permute-start | bytes 110600 | tf_op jit(solution)/shard_map/ppermute | solution.py:36
  56.4 3.9 %collective-permute-start.17 = (f32[8,128]{1,0:T(8,128)S(1)}, f32[8,128]{1,0:T(8,128)S(1)}, u32[]{:S(2)}, u32[]{:S(2)}) collective-permute-start(f32[8,128]{1,0:T(8,128)S(1)} %get-tuple-element.69), channel_id=1, source_target_pairs={{13,0},{12,1},{15,2},{14,3},{25,4},{24,5},{27,6},{26,7},{21,8},{20... | collective-permute-start | bytes 12296 | tf_op jit(solution)/shard_map/ppermute | solution.py:46
  56.4 3.9 %collective-permute-start.16 = (f32[8,128]{1,0:T(8,128)S(1)}, f32[8,128]{1,0:T(8,128)S(1)}, u32[]{:S(2)}, u32[]{:S(2)}) collective-permute-start(f32[8,128]{1,0:T(8,128)S(1)} %get-tuple-element.69), channel_id=1, source_target_pairs={{0,17},{1,16},{2,19},{3,18},{4,21},{5,20},{6,23},{7,22},{8,25},{9,... | collective-permute-start | bytes 12296 | tf_op jit(solution)/shard_map/ppermute | solution.py:56

commit v3 on v2

--- a/solution.py
+++ b/solution.py
@@ -327,7 +327,7 @@
     half_count, _, virt = lows[0].shape
     rows = virt // 2
     aux = near.shape[0]
-    group = max(g for g in range(2, 50, 2) if aux % g == 0)
+    group = max(g for g in range(2, 98, 2) if aux % g == 0)
     if own:
         out = (shaped(half_count, virt, virt), shaped(half_count, virt, virt, dtype=BF16))
     else:
@@ -350,7 +350,7 @@
             pltpu.VMEM((virt, half_count * virt), F32),
             pltpu.SemaphoreType.DMA(()),
         ),
-        limit=28,
+        limit=42,
         flops=8 * aux * half_count * virt**3,
     )
 
@@ -415,7 +415,7 @@
     packed[2 * half_count * single :, :] = sums
 
 
-def border_body(meta, picked, packed, came, whole, even_rows, odd_rows, sums, mate):
+def border_body(meta, picked, packed, came, whole, even_rows, odd_rows, mate):
     pairs, single, _ = whole.shape
     half_count = pairs // 2
     half = meta[2]
@@ -432,7 +432,6 @@
     for r in range(picked.shape[1]):
         even_rows[r * single : (r + 1) * single, :] = mate[picked[parity, r]]
         odd_rows[r * single : (r + 1) * single, :] = mate[picked[1 - parity, r]]
-    sums[...] = packed[2 * half_count * single :, :] + came[2 * half_count * single :, :]
 
 
 def close_body(meta, whole, even_came, odd_came, squares, new, norms):
@@ -592,9 +591,12 @@
     )
     last_came = swap(packed, 1)
     rows = shaped(border * row_count, virt)
-    whole, even_rows, odd_rows, sums = call(
+    sums = packed[pairs * row_count :] + last_came[pairs * row_count :]
+    cross = swap(sums, CROSS)
+    both_came = wide_swap(sums, 1, CROSS)
+    whole, even_rows, odd_rows = call(
         border_body,
-        (shaped(pairs, row_count, virt), rows, rows, small),
+        (shaped(pairs, row_count, virt), rows, rows),
         (SMEM, SMEM, VMEM, VMEM),
         meta,
         export_rows[0],
@@ -604,8 +606,6 @@
     )
     tail = border * row_count
     even_came = even_swap(jnp.concatenate([even_rows, sums], axis=0))
-    cross = swap(sums, CROSS)
-    both_came = wide_swap(sums, 1, CROSS)
     norm_squares = sums + cross
     sums = norm_squares + (even_came[tail:] + both_came)
     odd_came = odd_swap(jnp.concatenate([odd_rows, sums], axis=0), True)

time: 64.1 us -> 64.1 us (level)
  no operation moved by 1% of the time
where the time goes in v3:
time: 64.1 us; the launch traced here: 63.9 us
  Pallas kernels  30 us (47%)
  starting transfers between devices  15.9 us (25%)
  waiting for transfers between devices  14.8 us (23%)
  between operations  2.53 us (4%)
    pallas_call x9, Pallas kernels, call(): pl.pallas_call(body, out_shape=out_shape, in_specs=specs, out_specs=jax.t...  30 us
    ppermute x11, waiting for transfers between devices, swap(): return lax.ppermute(value, 'blk', [(at, at ^ step) for at in range(count)])  9.56 us
    ppermute x11, starting transfers between devices, swap(): return lax.ppermute(value, 'blk', [(at, at ^ step) for at in range(count)])  7.36 us
    ppermute x2, starting transfers between devices, odd_swap(): return lax.ppermute(value, ('frag', 'blk'), links)  4.31 us
    ppermute x4, starting transfers between devices, wide_swap(): return lax.ppermute(value, ('frag', 'blk'), links)  4.22 us
    ppermute x1, waiting for transfers between devices, odd_far_swap(): return lax.ppermute(value, ('frag', 'blk'), links)  3.03 us
    ppermute x4, waiting for transfers between devices, wide_swap(): return lax.ppermute(value, ('frag', 'blk'), links)  2.25 us
  transfers between devices with their start and end apart: 18, of which 6 were waited for; matrix products, arithmetic and copies ran while one was open for 0% of the time, Pallas kernels for 26%

profile of v3, /device:TPU:0, one launch (start us, length us, event | category | flops | bytes accessed | tf_op | source)
XLA Modules:
  0.0 63.9 jit_solution(8353929459893472016)
XLA Ops:
  0.6 0.6 collective-permute-start.3
  1.2 0.1 stack.23.meta
  1.3 1.7 %shard_map.112 = (bf16[4,32,128]{2,1,0:T(8,128)(2,1)S(1)}, bf16[4,32,128]{2,1,0:T(8,128)(2,1)S(1)}, f32[32,8,128]{2,1,0:T(8,128)S(1)}, f32[32,8,128]{2,1,0:T(8,1...) custom-call(s32[6]{0:T(128)S(1)} %stack.23.meta, ...), custom_call_target="tpu_custom_call" | custom-call | tf_op jit(solution)/shard_map/pallas_call | solution.py:64
  3.0 2.0 %shard_map.113 = (f32[12,32,128]{2,1,0:T(8,128)S(1)}, f32[16,32,128]{2,1,0:T(8,128)S(1)}, f32[128,128]{1,0:T(8,128)S(1)}, bf16[2,128,128]{2,1,0:T(8,128)(2,1)S(1)}, f32[8,32,128]{2,1,0:T(8,128)S(1)}) custom-call(s32[6]{0:T(128)S(1)} %stack.23.meta, f32[8,8]{1,0:T(8,128)S(1)} %get-tuple-element.36.occ, f32[1,8]{1,0:T(1,128)S(1)} %get-tuple-element.35.pair, ...), custom_call_target="tpu_custom_call" | custom-call | tf_op jit(solution)/shard_map/pallas_call | solution.py:64
  5.0 0.1 collective-permute-start.4
  5.1 2.9 %collective-permute-start.2 = (bf16[4,32,128]{2,1,0:T(8,128)(2,1)S(1)}, bf16[4,32,128]{2,1,0:T(8,128)(2,1)S(1)}, u32[]{:S(2)}, u32[]{:S(2)}) collective-permute-start(bf16[4,32,128]{2,1,0:T(8,128)(2,1)S(1)} %get-tuple-element.44), channel_id=1, source_target_pairs={{0,2},{1,3},{2,0},{3,1},{4,6},{5,7},{6,4},{7,5},{8,10},{9,11},{10,... | collective-permute-start | bytes 98312 | tf_op jit(solution)/shard_map/ppermute | solution.py:22
  8.0 0.0 collective-permute-start
  8.0 0.1 collective-permute-start.1
  8.1 0.0 collective-permute-done.4.rest_7_.came
  8.1 3.2 %collective-permute-done.1.rest_2_ = bf16[4,32,128]{2,1,0:T(8,128)(2,1)S(1)} collective-permute-done((bf16[4,32,128]{2,1,0:T(8,128)(2,1)S(1)}, bf16[4,32,128]{2,1,0:T(8,128)(2,1)S(1)}, u32[]{:S(2)}, u32[]{:S(2)}) %collective-permute-start.1) | collective-permute-done | bytes 32800 | tf_op jit(solution)/shard_map/ppermute | solution.py:22
  11.3 0.0 collective-permute-done.2.rest_3_
  11.3 0.0 collective-permute-done.rest_1_
  11.4 0.0 collective-permute-done.3.rest_5_.rest_2_
  11.4 11.0 %shard_map.114 = (f32[4,128,128]{2,1,0:T(8,128)S(1)}, bf16[4,128,128]{2,1,0:T(8,128)(2,1)S(1)}) custom-call(s32[6]{0:T(128)S(1)} %stack.23.meta, bf16[2,128,128]{2,1,0:T(8,128)(2,1)S(1)} %get-tuple-element.42.fock_low, bf16[4,32,128]{2,1,0:T(8,128)(2,1)S(1)} %get-tuple-element.43.rest_0_, bf16[4,32,128]{2,1,0:T(8,128)(2,1)S(1)} %collective-permute-done.rest_1_, ...), custom_call_target="tpu_custom_call" | custom-call | flops 6442450944 | tf_op jit(solution)/shard_map/pallas_call | solution.py:64
  22.4 0.6 collective-permute-start.5
  22.9 1.6 %collective-permute-start.8 = (f32[2,32,128]{2,1,0:T(8,128)S(1)}, f32[2,32,128]{2,1,0:T(8,128)S(1)}, u32[]{:S(2)}, u32[]{:S(2)}) collective-permute-start(f32[2,32,128]{2,1,0:T(8,128)S(1)} %get-tuple-element.56), channel_id=1, source_target_pairs={{0,5},{1,4},{2,7},{3,6},{4,1},{5,0},{6,3},{7,2},{8,13},{9,12},{10,... | collective-permute-start | bytes 98312 | tf_op jit(solution)/shard_map/ppermute | solution.py:56
  24.5 0.2 collective-permute-start.9
  24.7 2.8 %collective-permute-done.5.part_came = bf16[4,128,128]{2,1,0:T(8,128)(2,1)S(1)} collective-permute-done((bf16[4,128,128]{2,1,0:T(8,128)(2,1)S(1)}, bf16[4,128,128]{2,1,0:T(8,128)(2,1)S(1)}, u32[]{:S(2)}, u32[]{:S(2)}) %collective-permute-start.5) | collective-permute-done | bytes 131104 | tf_op jit(solution)/shard_map/ppermute | solution.py:22
  27.5 0.6 shard_map.115
  28.2 0.6 collective-permute-start.7
  28.7 11.2 %shard_map.116 = (bf16[4,64,128]{2,1,0:T(8,128)(2,1)S(1)}, f32[4,64,128]{2,1,0:T(8,128)S(1)}) custom-call(s32[6]{0:T(128)S(1)} %stack.23.meta, bf16[2,128,128]{2,1,0:T(8,128)(2,1)S(1)} %get-tuple-element.42.fock_low, bf16[4,128,128]{2,1,0:T(8,128)(2,1)S(1)} %get-tuple-element.51.rest_0_, bf16[96,128,128]{2,1,0:T(8,128)(2,1)} %bitcast.21, ...), custom_call_target="tpu_custom_call" | custom-call | flops 6442450944 | tf_op jit(solution)/shard_map/pallas_call | solution.py:64
  39.9 0.7 %collective-permute-start.6 = (bf16[4,64,128]{2,1,0:T(8,128)(2,1)S(1)}, bf16[4,64,128]{2,1,0:T(8,128)(2,1)S(1)}, u32[]{:S(2)}, u32[]{:S(2)}) collective-permute-start(bf16[4,64,128]{2,1,0:T(8,128)(2,1)S(1)} %get-tuple-element.53), channel_id=1, source_target_pairs={{0,3},{1,2},{2,1},{3,0},{4,7},{5,6},{6,5},{7,4},{8,11},{9,10},{10,... | collective-permute-start | bytes 196616 | tf_op jit(solution)/shard_map/ppermute | solution.py:22
  40.7 0.0 collective-permute-done.8.even_came
  40.7 0.0 collective-permute-done.9.odd_came
  40.7 0.0 collective-permute-done.7.from_mate
  40.7 0.0 copy-done
  40.7 1.0 %shard_map.117 = (f32[4,64,128]{2,1,0:T(8,128)S(1)}, f32[4,32,128]{2,1,0:T(8,128)S(1)}, f32[4,32,128]{2,1,0:T(8,128)S(1)}) custom-call(s32[6]{0:T(128)S(1)} %stack.23.meta, f32[8,8]{1,0:T(8,128)S(1)} %get-tuple-element.36.occ, f32[1,8]{1,0:T(1,128)S(1)} %get-tuple-element.35.pair, s32[2,2]{1,0:T(2,128)S(1)} %bitcast.13, ...), custom_call_target="tpu_custom_call" | custom-call | tf_op jit(solution)/shard_map/pallas_call | solution.py:64
  41.7 0.2 collective-permute-start.10
  41.9 2.3 %collective-permute-done.6.came = bf16[4,64,128]{2,1,0:T(8,128)(2,1)S(1)} collective-permute-done((bf16[4,64,128]{2,1,0:T(8,128)(2,1)S(1)}, bf16[4,64,128]{2,1,0:T(8,128)(2,1)S(1)}, u32[]{:S(2)}, u32[]{:S(2)}) %collective-permute-start.6) | collective-permute-done | bytes 65568 | tf_op jit(solution)/shard_map/ppermute | solution.py:22
  44.2 0.0 collective-permute-done.10.from_mate
  44.2 0.7 %shard_map.118.packed = f32[264,128]{1,0:T(8,128)S(1)} custom-call(s32[6]{0:T(128)S(1)} %stack.23.meta, f32[1,8]{1,0:T(1,128)S(1)} %get-tuple-element.35.pair, f32[4,64,128]{2,1,0:T(8,128)S(1)} %get-tuple-element.52.part, bf16[4,64,128]{2,1,0:T(8,128)(2,1)S(1)} %collective-permute-done.6.came, f32[128,128]{1,0:T(8,128)S(1)} %get-tuple-element.50.level, ...), custom_call_target="tpu_custom_call" | custom-call | tf_op jit(solution)/shard_map/pallas_call | solution.py:64
  44.9 0.2 collective-permute-start.11
  45.1 1.2 %collective-permute-done.11.came = f32[264,128]{1,0:T(8,128)S(1)} collective-permute-done((f32[264,128]{1,0:T(8,128)S(1)}, f32[264,128]{1,0:T(8,128)S(1)}, u32[]{:S(2)}, u32[]{:S(2)}) %collective-permute-start.11) | collective-permute-done | bytes 135200 | tf_op jit(solution)/shard_map/ppermute | solution.py:22
  46.3 0.6 shard_map.119
  46.9 1.3 %collective-permute-start.12 = (f32[72,128]{1,0:T(8,128)S(1)}, f32[72,128]{1,0:T(8,128)S(1)}, u32[]{:S(2)}, u32[]{:S(2)}) collective-permute-start(f32[72,128]{1,0:T(8,128)S(1)} %pad_maximum_fusion), channel_id=1, source_target_pairs={{0,5},{1,4},{2,7},{3,6},{4,1},{5,0},{6,3},{7,2},{8,13},{9,12},{10,... | collective-permute-start | bytes 110600 | tf_op jit(solution)/shard_map/ppermute | solution.py:56
  48.3 0.4 collective-permute-start.14
  48.7 1.3 %collective-permute-start.13 = (f32[8,128]{1,0:T(8,128)S(1)}, f32[8,128]{1,0:T(8,128)S(1)}, u32[]{:S(2)}, u32[]{:S(2)}) collective-permute-start(f32[8,128]{1,0:T(8,128)S(1)} %slice_add_fusion.2), channel_id=1, source_target_pairs={{0,3},{1,2},{2,1},{3,0},{4,7},{5,6},{6,5},{7,4},{8,11},{9,10},{10,... | collective-permute-start | bytes 12296 | tf_op jit(solution)/shard_map/ppermute | solution.py:22
  50.0 2.2 %collective-permute-done.14 = f32[8,128]{1,0:T(8,128)S(1)} collective-permute-done((f32[8,128]{1,0:T(8,128)S(1)}, f32[8,128]{1,0:T(8,128)S(1)}, u32[]{:S(2)}, u32[]{:S(2)}) %collective-permute-start.14) | collective-permute-done | bytes 4128 | tf_op jit(solution)/shard_map/ppermute | solution.py:56
  52.2 0.0 collective-permute-done.13
  52.2 0.0 collective-permute-done.12.even_came
  52.2 4.1 %collective-permute-start.15 = (f32[72,128]{1,0:T(8,128)S(1)}, f32[72,128]{1,0:T(8,128)S(1)}, u32[]{:S(2)}, u32[]{:S(2)}) collective-permute-start(f32[72,128]{1,0:T(8,128)S(1)} %pad_maximum_fusion.1), channel_id=1, source_target_pairs={{0,29},{1,28},{2,31},{3,30},{4,9},{5,8},{6,11},{7,10},{8,5},{9,4},... | collective-permute-start | bytes 110600 | tf_op jit(solution)/shard_map/ppermute | solution.py:36
  56.4 0.0 collective-permute-start.17
  56.4 0.9 %collective-permute-start.16 = (f32[8,128]{1,0:T(8,128)S(1)}, f32[8,128]{1,0:T(8,128)S(1)}, u32[]{:S(2)}, u32[]{:S(2)}) collective-permute-start(f32[8,128]{1,0:T(8,128)S(1)} %get-tuple-element.67), channel_id=1, source_target_pairs={{0,17},{1,16},{2,19},{3,18},{4,21},{5,20},{6,23},{7,22},{8,25},{9,... | collective-permute-start | bytes 12296 | tf_op jit(solution)/shard_map/ppermute | solution.py:56
  57.3 3.0 %collective-permute-done.17 = f32[8,128]{1,0:T(8,128)S(1)} collective-permute-done((f32[8,128]{1,0:T(8,128)S(1)}, f32[8,128]{1,0:T(8,128)S(1)}, u32[]{:S(2)}, u32[]{:S(2)}) %collective-permute-start.17) | collective-permute-done | bytes 4128 | tf_op jit(solution)/shard_map/ppermute | solution.py:46
  60.3 0.0 collective-permute-done.16
  60.3 0.0 collective-permute-done.15.odd_came
  60.3 0.5 slice.27
  61.5 1.3 %shard_map.120 = (f32[32,8,128]{2,1,0:T(8,128)}, f32[1,2]{1,0:T(1,128)}) custom-call(s32[6]{0:T(128)S(1)} %stack.23.meta, f32[8,32,128]{2,1,0:T(8,128)S(1)} %get-tuple-element.62.whole, f32[72,128]{1,0:T(8,128)S(1)} %collective-permute-done.12.even_came, f32[72,128]{1,0:T(8,128)S(1)} %collective-permute-done.15.odd_came, f32[8,128]{1,0:T(8,128)S(1)} %get-tuple-element.68.squares), custom_call_target="tpu_custom_call" | custom-call | tf_op jit(solution)/shard_map/pallas_call | solution.py:64
  (7 shorter events, 0.0 us)
Async XLA Ops:
  0.6 10.7 %collective-permute-start.3 = (bf16[96,128,128]{2,1,0:T(8,128)(2,1)}, bf16[96,128,128]{2,1,0:T(8,128)(2,1)S(1)}, u32[]{:S(2)}, u32[]{:S(2)}) collective-permute-start(bf16[96,128,128]{2,1,0:T(8,128)(2,1)} %bitcast.19), channel_id=1, source_target_pairs={{0,1},{1,0},{2,3},{3,2},{4,5},{5,4},{6,7},{7,6},{8,9},{9,8},{10,11... | collective-permute-start | bytes 9437192 | tf_op jit(solution)/shard_map/ppermute | solution.py:22
  5.0 3.2 %collective-permute-start.4 = (f32[16,32,128]{2,1,0:T(8,128)S(1)}, f32[16,32,128]{2,1,0:T(8,128)S(1)}, u32[]{:S(2)}, u32[]{:S(2)}) collective-permute-start(f32[16,32,128]{2,1,0:T(8,128)S(1)} %get-tuple-element.46), channel_id=1, source_target_pairs={{0,1},{1,0},{2,3},{3,2},{4,5},{5,4},{6,7},{7,6},{8,9},{9,8},{10,11... | collective-permute-start | bytes 786440 | tf_op jit(solution)/shard_map/ppermute | solution.py:22
  5.1 6.3 %collective-permute-start.2 = (bf16[4,32,128]{2,1,0:T(8,128)(2,1)S(1)}, bf16[4,32,128]{2,1,0:T(8,128)(2,1)S(1)}, u32[]{:S(2)}, u32[]{:S(2)}) collective-permute-start(bf16[4,32,128]{2,1,0:T(8,128)(2,1)S(1)} %get-tuple-element.44), channel_id=1, source_target_pairs={{0,2},{1,3},{2,0},{3,1},{4,6},{5,7},{6,4},{7,5},{8,10},{9,11},{10,... | collective-permute-start | bytes 98312 | tf_op jit(solution)/shard_map/ppermute | solution.py:22
  8.0 3.3 %collective-permute-start = (bf16[4,32,128]{2,1,0:T(8,128)(2,1)S(1)}, bf16[4,32,128]{2,1,0:T(8,128)(2,1)S(1)}, u32[]{:S(2)}, u32[]{:S(2)}) collective-permute-start(bf16[4,32,128]{2,1,0:T(8,128)(2,1)S(1)} %get-tuple-element.44), channel_id=1, source_target_pairs={{0,1},{1,0},{2,3},{3,2},{4,5},{5,4},{6,7},{7,6},{8,9},{9,8},{10,11... | collective-permute-start | bytes 98312 | tf_op jit(solution)/shard_map/ppermute | solution.py:22
  8.0 3.3 %collective-permute-start.1 = (bf16[4,32,128]{2,1,0:T(8,128)(2,1)S(1)}, bf16[4,32,128]{2,1,0:T(8,128)(2,1)S(1)}, u32[]{:S(2)}, u32[]{:S(2)}) collective-permute-start(bf16[4,32,128]{2,1,0:T(8,128)(2,1)S(1)} %get-tuple-element.43.rest_0_), channel_id=1, source_target_pairs={{0,3},{1,2},{2,1},{3,0},{4,7},{5,6},{6,5},{7,4},{8,11},{9,10},{10,... | collective-permute-start | bytes 98312 | tf_op jit(solution)/shard_map/ppermute | solution.py:22
  22.4 5.2 %collective-permute-start.5 = (bf16[4,128,128]{2,1,0:T(8,128)(2,1)S(1)}, bf16[4,128,128]{2,1,0:T(8,128)(2,1)S(1)}, u32[]{:S(2)}, u32[]{:S(2)}) collective-permute-start(bf16[4,128,128]{2,1,0:T(8,128)(2,1)S(1)} %get-tuple-element.49), channel_id=1, source_target_pairs={{0,3},{1,2},{2,1},{3,0},{4,7},{5,6},{6,5},{7,4},{8,11},{9,10},{10,... | collective-permute-start | bytes 393224 | tf_op jit(solution)/shard_map/ppermute | solution.py:22
  22.9 17.7 %collective-permute-start.8 = (f32[2,32,128]{2,1,0:T(8,128)S(1)}, f32[2,32,128]{2,1,0:T(8,128)S(1)}, u32[]{:S(2)}, u32[]{:S(2)}) collective-permute-start(f32[2,32,128]{2,1,0:T(8,128)S(1)} %get-tuple-element.56), channel_id=1, source_target_pairs={{0,5},{1,4},{2,7},{3,6},{4,1},{5,0},{6,3},{7,2},{8,13},{9,12},{10,... | collective-permute-start | bytes 98312 | tf_op jit(solution)/shard_map/ppermute | solution.py:56
  24.5 16.1 %collective-permute-start.9 = (f32[2,32,128]{2,1,0:T(8,128)S(1)}, f32[2,32,128]{2,1,0:T(8,128)S(1)}, u32[]{:S(2)}, u32[]{:S(2)}) collective-permute-start(f32[2,32,128]{2,1,0:T(8,128)S(1)} %get-tuple-element.57), channel_id=1, source_target_pairs={{0,1},{1,0},{2,3},{3,2},{4,9},{5,8},{6,11},{7,10},{8,5},{9,4},{10,... | collective-permute-start | bytes 98312 | tf_op jit(solution)/shard_map/ppermute | solution.py:36
  28.2 12.5 %collective-permute-start.7 = (f32[4,64,128]{2,1,0:T(8,128)S(1)}, f32[4,64,128]{2,1,0:T(8,128)S(1)}, u32[]{:S(2)}, u32[]{:S(2)}) collective-permute-start(f32[4,64,128]{2,1,0:T(8,128)S(1)} %get-tuple-element.54.amp), channel_id=1, source_target_pairs={{0,1},{1,0},{2,3},{3,2},{4,5},{5,4},{6,7},{7,6},{8,9},{9,8},{10,11... | collective-permute-start | bytes 393224 | tf_op jit(solution)/shard_map/ppermute | solution.py:22
  28.7 11.9 %copy-start = (s32[1,2,2]{2,1,0:T(2,128)S(1)}, s32[1,2,2]{2,1,0:T(2,128)}, u32[]{:S(2)}) copy-start(s32[1,2,2]{2,1,0:T(2,128)} %param.17) | copy-start | bytes 52
  39.9 4.3 %collective-permute-start.6 = (bf16[4,64,128]{2,1,0:T(8,128)(2,1)S(1)}, bf16[4,64,128]{2,1,0:T(8,128)(2,1)S(1)}, u32[]{:S(2)}, u32[]{:S(2)}) collective-permute-start(bf16[4,64,128]{2,1,0:T(8,128)(2,1)S(1)} %get-tuple-element.53), channel_id=1, source_target_pairs={{0,3},{1,2},{2,1},{3,0},{4,7},{5,6},{6,5},{7,4},{8,11},{9,10},{10,... | collective-permute-start | bytes 196616 | tf_op jit(solution)/shard_map/ppermute | solution.py:22
  41.7 2.5 %collective-permute-start.10 = (f32[4,32,128]{2,1,0:T(8,128)S(1)}, f32[4,32,128]{2,1,0:T(8,128)S(1)}, u32[]{:S(2)}, u32[]{:S(2)}) collective-permute-start(f32[4,32,128]{2,1,0:T(8,128)S(1)} %get-tuple-element.60), channel_id=1, source_target_pairs={{0,1},{1,0},{2,3},{3,2},{4,5},{5,4},{6,7},{7,6},{8,9},{9,8},{10,11... | collective-permute-start | bytes 196616 | tf_op jit(solution)/shard_map/ppermute | solution.py:22
  44.9 1.4 %collective-permute-start.11 = (f32[264,128]{1,0:T(8,128)S(1)}, f32[264,128]{1,0:T(8,128)S(1)}, u32[]{:S(2)}, u32[]{:S(2)}) collective-permute-start(f32[264,128]{1,0:T(8,128)S(1)} %shard_map.118.packed), channel_id=1, source_target_pairs={{0,1},{1,0},{2,3},{3,2},{4,5},{5,4},{6,7},{7,6},{8,9},{9,8},{10,11... | collective-permute-start | bytes 405512 | tf_op jit(solution)/shard_map/ppermute | solution.py:22
  46.9 5.3 %collective-permute-start.12 = (f32[72,128]{1,0:T(8,128)S(1)}, f32[72,128]{1,0:T(8,128)S(1)}, u32[]{:S(2)}, u32[]{:S(2)}) collective-permute-start(f32[72,128]{1,0:T(8,128)S(1)} %pad_maximum_fusion), channel_id=1, source_target_pairs={{0,5},{1,4},{2,7},{3,6},{4,1},{5,0},{6,3},{7,2},{8,13},{9,12},{10,... | collective-permute-start | bytes 110600 | tf_op jit(solution)/shard_map/ppermute | solution.py:56
  48.3 3.9 %collective-permute-start.14 = (f32[8,128]{1,0:T(8,128)S(1)}, f32[8,128]{1,0:T(8,128)S(1)}, u32[]{:S(2)}, u32[]{:S(2)}) collective-permute-start(f32[8,128]{1,0:T(8,128)S(1)} %slice_add_fusion.2), channel_id=1, source_target_pairs={{0,7},{1,6},{2,5},{3,4},{4,3},{5,2},{6,1},{7,0},{8,15},{9,14},{10,... | collective-permute-start | bytes 12296 | tf_op jit(solution)/shard_map/ppermute | solution.py:56
  48.7 3.6 %collective-permute-start.13 = (f32[8,128]{1,0:T(8,128)S(1)}, f32[8,128]{1,0:T(8,128)S(1)}, u32[]{:S(2)}, u32[]{:S(2)}) collective-permute-start(f32[8,128]{1,0:T(8,128)S(1)} %slice_add_fusion.2), channel_id=1, source_target_pairs={{0,3},{1,2},{2,1},{3,0},{4,7},{5,6},{6,5},{7,4},{8,11},{9,10},{10,... | collective-permute-start | bytes 12296 | tf_op jit(solution)/shard_map/ppermute | solution.py:22
  52.2 8.1 %collective-permute-start.15 = (f32[72,128]{1,0:T(8,128)S(1)}, f32[72,128]{1,0:T(8,128)S(1)}, u32[]{:S(2)}, u32[]{:S(2)}) collective-permute-start(f32[72,128]{1,0:T(8,128)S(1)} %pad_maximum_fusion.1), channel_id=1, source_target_pairs={{0,29},{1,28},{2,31},{3,30},{4,9},{5,8},{6,11},{7,10},{8,5},{9,4},... | collective-permute-start | bytes 110600 | tf_op jit(solution)/shard_map/ppermute | solution.py:36
  56.4 3.9 %collective-permute-start.17 = (f32[8,128]{1,0:T(8,128)S(1)}, f32[8,128]{1,0:T(8,128)S(1)}, u32[]{:S(2)}, u32[]{:S(2)}) collective-permute-start(f32[8,128]{1,0:T(8,128)S(1)} %get-tuple-element.67), channel_id=1, source_target_pairs={{13,0},{12,1},{15,2},{14,3},{25,4},{24,5},{27,6},{26,7},{21,8},{20... | collective-permute-start | bytes 12296 | tf_op jit(solution)/shard_map/ppermute | solution.py:46
  56.4 3.9 %collective-permute-start.16 = (f32[8,128]{1,0:T(8,128)S(1)}, f32[8,128]{1,0:T(8,128)S(1)}, u32[]{:S(2)}, u32[]{:S(2)}) collective-permute-start(f32[8,128]{1,0:T(8,128)S(1)} %get-tuple-element.67), channel_id=1, source_target_pairs={{0,17},{1,16},{2,19},{3,18},{4,21},{5,20},{6,23},{7,22},{8,25},{9,... | collective-permute-start | bytes 12296 | tf_op jit(solution)/shard_map/ppermute | solution.py:56
